TPU v7x, 32 devices: a whole 2x2x4 slice. The times are simulated.
32 devices in a mesh: freq: 2 (over x), leaf: 16 (over z, y, core).
Axes of the slice: x: 2, y: 2, z: 4, core: 2. Of those that a mesh axis runs over, the one named last changes fastest.
Arguments:
- rhs: float32 [128, 256, 128], P(('freq', 'leaf')), parts along dimension 0, may hold values from -6 to 6
- leaf_q: float32 [128, 256, 256], P(('freq', 'leaf')), parts along dimension 0, may hold values from -0.375 to 0.375
- leaf_e: float32 [128, 256, 256], P(('freq', 'leaf')), parts along dimension 0, may hold values from -0.375 to 0.375
- leaf_w: float32 [128, 256, 128], P(('freq', 'leaf')), parts along dimension 0, may hold values from -0.375 to 0.375
- node_q: float32 [96, 256, 256], P(('freq', 'leaf')), parts along dimension 0, may hold values from -0.375 to 0.375
- node_e: float32 [96, 256, 256], P(('freq', 'leaf')), parts along dimension 0, may hold values from -0.375 to 0.375
- node_w: float32 [96, 256, 128], P(('freq', 'leaf')), parts along dimension 0, may hold values from -0.375 to 0.375
- top_q: float32 [128, 256, 256], P(('freq', 'leaf')), parts along dimension 0, as said below
- top_e: float32 [128, 256, 256], P(('freq', 'leaf')), parts along dimension 0, as said below
- top_w: float32 [128, 256, 128], P(('freq', 'leaf')), parts along dimension 0, as said below
Outputs:
- solution: float32 [128, 256, 128], P(('freq', 'leaf')), parts along dimension 0
There are 2 independent parts, one for each index of `freq`. A program takes and returns all parts, laid end to end along the dimension named above; each array names one. Nothing has to cross between parts.
Inputs may be any that keep to these rules, and one draw needn't show every extreme that they name: Device d's 4 rows of top_q hold, in row l-1, the transform of the level l node d // 2^l; devices with equal d // 2^l hold equal rows l-1. `top_e`: likewise for the inverted blocks: row l-1 of device d belongs to node d // 2^l of level l and is equal on all devices of that node. `top_w`: likewise for the generators: row l-1 of device d belongs to node d // 2^l of level l and is equal on all devices of that node.
All inputs are finite; a program needn't handle non-finite values.
Results may differ from a plain program's by a relative error of at most 0.00012.
Values sent between devices are 32-bit elements; how exact they have to be, the bound alone decides.
No kernel may reach another device: no remote copies, remote signals or barrier semaphores. Data moves between devices by JAX's collectives and lax.ppermute only.
A program may use at most 64 MiB of HBM per device.

v0:
```python
import jax
import jax.numpy as jnp
from jax import lax
from jax.sharding import PartitionSpec as P

HIGH = lax.Precision.HIGHEST


def swapped(value, axis, apart):
    mask = 2**apart
    pairs = [(source, source ^ mask) for source in range(lax.axis_size(axis))]
    return lax.ppermute(value, axis, pairs)


def batched(mats, vecs):
    return jnp.einsum("nij,njr->nir", mats, vecs, precision=HIGH)


def batched_t(mats, vecs):
    return jnp.einsum("nji,njr->nir", mats, vecs, precision=HIGH)


def upward(qmat, emat, wmat, vecs):
    values = batched(emat, batched(qmat, vecs))
    return (values, batched_t(wmat, values))


def downward(qmat, emat, wmat, values, parent):
    return batched_t(qmat, values - batched(emat, batched(wmat, parent)))


def pick_level(gens, level, leaf_count):
    count = leaf_count // 2**level
    offset = leaf_count - 2 * count
    return gens[offset : offset + count]


def tree_sweep(reduced, top_q, top_e, top_w, width):
    parts = lax.axis_size("leaf")
    position = lax.axis_index("leaf")
    levels = parts.bit_length() - 1
    upper_values = []
    for level in range(1, levels + 1):
        other = swapped(reduced, "leaf", level - 1)
        on_right = position // 2 ** (level - 1) % 2 == 1
        stacked = jnp.where(
            on_right,
            jnp.concatenate([other, reduced], axis=1),
            jnp.concatenate([reduced, other], axis=1),
        )
        values, reduced = upward(
            top_q[level - 1 : level], top_e[level - 1 : level], top_w[level - 1 : level], stacked
        )
        upper_values.append(values)
    answer = upper_values[-1]
    parent = answer[:, :width]
    for level in range(levels, 0, -1):
        on_right = position // 2 ** (level - 1) % 2 == 1
        parent = jnp.where(on_right, answer[:, width:], answer[:, :width])
        if level > 1:
            answer = downward(
                top_q[level - 2 : level - 1],
                top_e[level - 2 : level - 1],
                top_w[level - 2 : level - 1],
                upper_values[level - 2],
                parent,
            )
    return parent


def body(rhs, leaf_q, leaf_e, leaf_w, node_q, node_e, node_w, top_q, top_e, top_w):
    width = leaf_w.shape[2]
    cols = rhs.shape[2]
    leaf_count = rhs.shape[0]
    local_levels = leaf_count.bit_length() - 1
    values, reduced = upward(leaf_q, leaf_e, leaf_w, rhs)
    local_values = [values]
    for level in range(1, local_levels + 1):
        stacked = reduced.reshape(-1, 2 * width, cols)
        values, reduced = upward(
            pick_level(node_q, level, leaf_count),
            pick_level(node_e, level, leaf_count),
            pick_level(node_w, level, leaf_count),
            stacked,
        )
        local_values.append(values)
    half = cols // 2
    first = tree_sweep(reduced[:, :, :half], top_q, top_e, top_w, width)
    second = tree_sweep(reduced[:, :, half:], top_q, top_e, top_w, width)
    parent = jnp.concatenate([first, second], axis=2)
    for level in range(local_levels, 0, -1):
        answer = downward(
            pick_level(node_q, level, leaf_count),
            pick_level(node_e, level, leaf_count),
            pick_level(node_w, level, leaf_count),
            local_values[level],
            parent,
        )
        parent = answer.reshape(-1, width, cols)
    return downward(leaf_q, leaf_e, leaf_w, local_values[0], parent)


def solution(mesh):
    in_specs = (
        P(("freq", "leaf"), None, None),
        P(("freq", "leaf"), None, None),
        P(("freq", "leaf"), None, None),
        P(("freq", "leaf"), None, None),
        P(("freq", "leaf"), None, None),
        P(("freq", "leaf"), None, None),
        P(("freq", "leaf"), None, None),
        P(("freq", "leaf"), None, None),
        P(("freq", "leaf"), None, None),
        P(("freq", "leaf"), None, None),
    )
    out_specs = P(("freq", "leaf"), None, None)
    return jax.shard_map(body, mesh=mesh, in_specs=in_specs, out_specs=out_specs, check_vma=False)
```

profile of v0, /device:TPU:0, one launch (start us, length us, event | category | flops | bytes accessed | tf_op | source)
XLA Modules:
  0.0 45.8 jit_solution(10212250054275632589)
XLA Ops:
  0.0 2.7 %fusion.218 = f32[4,256,128]{1,2,0:T(8,128)S(1)} fusion(f32[4,256,256]{2,1,0:T(8,128)} %param.11, f32[4,256,128]{2,1,0:T(8,128)} %param.10), kind=kOutput, calls=%fused_computation.253 | convolution fusion | flops 402653184 | bytes 2097152 | tf_op jit(solution)/shard_map/nij,njr->nir/dot_general | solution.py:16
  2.7 1.2 %fusion.219 = f32[4,128,256]{2,1,0:T(8,128)S(1)} fusion(f32[4,256,128]{1,2,0:T(8,128)S(1)} %fusion.218, f32[4,256,256]{2,1,0:T(8,128)S(1)} %copy-done), kind=kOutput, calls=%fused_computation.254 | convolution fusion | flops 402653184 | bytes 2097152 | tf_op jit(solution)/shard_map/nij,njr->nir/dot_general | solution.py:16
  3.9 1.0 %fusion.220 = f32[4,128,128]{1,2,0:T(8,128)S(1)} fusion(f32[4,128,256]{2,1,0:T(8,128)S(1)} %fusion.219, f32[4,256,128]{2,1,0:T(8,128)S(1)} %copy-done.11), kind=kOutput, calls=%fused_computation.255 | convolution fusion | flops 201326592 | bytes 1310720 | tf_op jit(solution)/shard_map/nji,njr->nir/dot_general | solution.py:20
  5.2 0.7 %fusion.5 = f32[2,128,256]{2,1,0:T(8,128)S(1)} fusion(f32[2,256,128]{2,1,0:T(8,128)S(1)} %bitcast.265, f32[3,256,256]{2,1,0:T(8,128)S(1)} %copy-done.9), kind=kOutput, calls=%fused_computation.25 | convolution fusion | flops 201326592 | bytes 1048576 | tf_op jit(solution)/shard_map/nij,njr->nir/dot_general | solution.py:16
  6.2 0.6 %fusion.2 = f32[2,128,256]{2,1,0:T(8,128)S(1)} fusion(f32[2,128,256]{2,1,0:T(8,128)S(1)} %fusion.5, f32[3,256,256]{2,1,0:T(8,128)S(1)} %copy-done.7), kind=kOutput, calls=%fused_computation.22 | convolution fusion | flops 201326592 | bytes 1048576 | tf_op jit(solution)/shard_map/nij,njr->nir/dot_general | solution.py:16
  7.2 0.6 %fusion.64 = f32[2,128,128]{1,2,0:T(8,128)S(1)} fusion(f32[2,128,256]{2,1,0:T(8,128)S(1)} %fusion.2, f32[3,256,128]{2,1,0:T(8,128)S(1)} %copy-done.13), kind=kOutput, calls=%fused_computation.85 | convolution fusion | flops 100663296 | bytes 655360 | tf_op jit(solution)/shard_map/nji,njr->nir/dot_general | solution.py:20
  8.9 0.7 %fusion.217 = (f32[1,128,64]{1,2,0:T(8,128)}, f32[128,64]{0,1:T(8,128)}, f32[128,64]{0,1:T(8,128)}, f32[1,128,64]{1,2,0:T(8,128)}) fusion(f32[1,128,128]{1,2,0:T(8,128)S(1)} %convolution_bitcast_fusion.10), kind=kLoop, calls=%fused_computation.252 | loop fusion | bytes 196608 | tf_op jit(solution)/shard_map/slice | solution.py:88
  10.1 1.2 %collective-permute-done = f32[1,128,64]{1,2,0:T(8,128)} collective-permute-done((f32[1,128,64]{1,2,0:T(8,128)}, f32[1,128,64]{1,2,0:T(8,128)}, u32[]{:S(2)}, u32[]{:S(2)}) %collective-permute-start) | collective-permute-done | bytes 32800 | tf_op jit(solution)/shard_map/ppermute | solution.py:12
  11.3 1.2 %fusion.50 = f32[64,256]{1,0:T(8,128)S(1)} fusion(f32[4,256,256]{2,1,0:T(8,128)S(1)} %copy-done.2, f32[128,64]{0,1:T(8,128)} %get-tuple-element.6, f32[128,64]{0,1:T(8,128)} %bitcast.9, pred[]{:T(512)S(6)} %eq.41), kind=kOutput, calls=%fused_computation.70 | convolution fusion | flops 50380800 | bytes 393217 | tf_op jit(solution)/shard_map/nij,njr->nir/dot_general | solution.py:16
  13.1 2.9 %collective-permute-start.1 = (f32[1,128,64]{1,2,0:T(8,128)S(1)}, f32[1,128,64]{1,2,0:T(8,128)S(1)}, u32[]{:S(2)}, u32[]{:S(2)}) collective-permute-start(f32[1,128,64]{1,2,0:T(8,128)S(1)} %bitcast.270), channel_id=1, source_target_pairs={{0,2},{1,3},{2,0},{3,1},{4,6},{5,7},{6,4},{7,5},{8,10},{9,11},{10,... | collective-permute-start | bytes 98312 | tf_op jit(solution)/shard_map/ppermute | solution.py:12
  16.0 1.2 %fusion.47 = f32[64,256]{1,0:T(8,128)S(1)} fusion(f32[4,256,256]{2,1,0:T(8,128)S(1)} %copy-done.2, f32[128,64]{0,1:T(8,128)S(1)} %copy-done.15, f32[128,64]{0,1:T(8,128)} %bitcast.47, pred[]{:T(512)S(6)} %eq.41), kind=kOutput, calls=%fused_computation.67 | convolution fusion | flops 50380800 | bytes 393217 | tf_op jit(solution)/shard_map/nij,njr->nir/dot_general | solution.py:16
  17.8 0.5 %collective-permute-start.5 = (f32[1,128,64]{1,2,0:T(8,128)S(1)}, f32[1,128,64]{1,2,0:T(8,128)S(1)}, u32[]{:S(2)}, u32[]{:S(2)}) collective-permute-start(f32[1,128,64]{1,2,0:T(8,128)S(1)} %bitcast.272), channel_id=1, source_target_pairs={{0,2},{1,3},{2,0},{3,1},{4,6},{5,7},{6,4},{7,5},{8,10},{9,11},{10,... | collective-permute-start | bytes 98312 | tf_op jit(solution)/shard_map/ppermute | solution.py:12
  19.3 1.7 %collective-permute-start.2 = (f32[1,128,64]{1,2,0:T(8,128)S(1)}, f32[1,128,64]{1,2,0:T(8,128)S(1)}, u32[]{:S(2)}, u32[]{:S(2)}) collective-permute-start(f32[1,128,64]{1,2,0:T(8,128)S(1)} %bitcast.274), channel_id=1, source_target_pairs={{0,4},{1,5},{2,6},{3,7},{4,0},{5,1},{6,2},{7,3},{8,12},{9,13},{10,... | collective-permute-start | bytes 98312 | tf_op jit(solution)/shard_map/ppermute | solution.py:12
  21.0 0.8 %collective-permute-done.5 = f32[1,128,64]{1,2,0:T(8,128)S(1)} collective-permute-done((f32[1,128,64]{1,2,0:T(8,128)S(1)}, f32[1,128,64]{1,2,0:T(8,128)S(1)}, u32[]{:S(2)}, u32[]{:S(2)}) %collective-permute-start.5) | collective-permute-done | bytes 32800 | tf_op jit(solution)/shard_map/ppermute | solution.py:12
  22.8 1.6 %collective-permute-start.6 = (f32[1,128,64]{1,2,0:T(8,128)S(1)}, f32[1,128,64]{1,2,0:T(8,128)S(1)}, u32[]{:S(2)}, u32[]{:S(2)}) collective-permute-start(f32[1,128,64]{1,2,0:T(8,128)S(1)} %bitcast.276), channel_id=1, source_target_pairs={{0,4},{1,5},{2,6},{3,7},{4,0},{5,1},{6,2},{7,3},{8,12},{9,13},{10,... | collective-permute-start | bytes 98312 | tf_op jit(solution)/shard_map/ppermute | solution.py:12
  25.4 2.7 %collective-permute-start.3 = (f32[1,128,64]{1,2,0:T(8,128)S(1)}, f32[1,128,64]{1,2,0:T(8,128)S(1)}, u32[]{:S(2)}, u32[]{:S(2)}) collective-permute-start(f32[1,128,64]{1,2,0:T(8,128)S(1)} %bitcast.278), channel_id=1, source_target_pairs={{0,8},{1,9},{2,10},{3,11},{4,12},{5,13},{6,14},{7,15},{8,0},{9,1},... | collective-permute-start | bytes 98312 | tf_op jit(solution)/shard_map/ppermute | solution.py:12
  29.0 1.4 %collective-permute-start.7 = (f32[1,128,64]{1,2,0:T(8,128)S(1)}, f32[1,128,64]{1,2,0:T(8,128)S(1)}, u32[]{:S(2)}, u32[]{:S(2)}) collective-permute-start(f32[1,128,64]{1,2,0:T(8,128)S(1)} %bitcast.268), channel_id=1, source_target_pairs={{0,8},{1,9},{2,10},{3,11},{4,12},{5,13},{6,14},{7,15},{8,0},{9,1},... | collective-permute-start | bytes 98312 | tf_op jit(solution)/shard_map/ppermute | solution.py:12
  34.2 0.5 %fusion.12 = f32[64,256]{1,0:T(8,128)S(1)} fusion(f32[4,256,256]{2,1,0:T(8,128)S(1)} %copy-done.2, f32[128,64]{0,1:T(8,128)S(1)} %bitcast.269, f32[128,64]{0,1:T(8,128)S(1)} %bitcast.280, pred[]{:T(512)S(6)} %eq.44), kind=kOutput, calls=%fused_computation.32 | convolution fusion | flops 50380800 | bytes 393217 | tf_op jit(solution)/shard_map/nij,njr->nir/dot_general | solution.py:16
  39.7 0.6 %convolution_subtract_fusion.1 = f32[2,128,256]{2,1,0:T(8,128)S(1)} fusion(f32[2,128,256]{2,1,0:T(8,128)S(1)} %fusion.2, f32[2,128,256]{2,1,0:T(8,128)S(1)} %fusion.66, f32[3,256,256]{2,1,0:T(8,128)S(1)} %copy-done.8), kind=kOutput, calls=%fused_computation.3 | convolution fusion | flops 201392128 | bytes 1310720 | tf_op jit(solution)/shard_map/nij,njr->nir/dot_general | solution.py:16
  40.9 0.9 %copy-done.12 = f32[4,256,128]{2,1,0:T(8,128)S(1)} copy-done((f32[4,256,128]{2,1,0:T(8,128)S(1)}, f32[4,256,128]{2,1,0:T(8,128)}, u32[]{:S(2)}) %copy-start.12) | copy-done | bytes 524312
  41.8 0.6 %fusion.221 = f32[4,128,256]{2,1,0:T(8,128)S(1)} fusion(f32[4,128,128]{2,1,0:T(8,128)S(1)} %bitcast.264, f32[4,256,128]{2,1,0:T(8,128)S(1)} %copy-done.12), kind=kOutput, calls=%fused_computation.256 | convolution fusion | flops 201326592 | bytes 1310720 | tf_op jit(solution)/shard_map/nij,njr->nir/dot_general | solution.py:16
  42.9 1.2 %convolution_subtract_fusion = f32[4,128,256]{2,1,0:T(8,128)S(1)} fusion(f32[4,128,256]{2,1,0:T(8,128)S(1)} %copy-done.5, f32[4,128,256]{2,1,0:T(8,128)S(1)} %fusion.221, f32[4,256,256]{2,1,0:T(8,128)S(1)} %copy-done), kind=kOutput, calls=%fused_computation | convolution fusion | flops 402784256 | bytes 2621440 | tf_op jit(solution)/shard_map/nij,njr->nir/dot_general | solution.py:16
  44.1 0.8 %convolution_bitcast_fusion = f32[4,256,128]{1,2,0:T(8,128)S(1)} fusion(f32[4,128,256]{2,1,0:T(8,128)S(1)} %convolution_subtract_fusion, f32[4,256,256]{2,1,0:T(8,128)S(1)} %copy-done.6), kind=kOutput, calls=%fused_computation.1 | convolution fusion | flops 402653184 | bytes 2097152 | tf_op jit(solution)/shard_map/nji,njr->nir/dot_general | solution.py:20
  44.8 1.0 %copy.17 = f32[4,256,128]{2,1,0:T(8,128)} copy(f32[4,256,128]{1,2,0:T(8,128)S(1)} %convolution_bitcast_fusion) | data formatting | bytes 1048576 | tf_op jit(solution)/shard_map/nji,njr->nir/dot_general | solution.py:20
  (87 shorter events, 17.1 us)
Async XLA Ops:
  0.0 2.7 %copy-start = (f32[4,256,256]{2,1,0:T(8,128)S(1)}, f32[4,256,256]{2,1,0:T(8,128)}, u32[]{:S(2)}) copy-start(f32[4,256,256]{2,1,0:T(8,128)} %param.12) | copy-start | bytes 3145732
  2.7 1.2 %copy-start.11 = (f32[4,256,128]{2,1,0:T(8,128)S(1)}, f32[4,256,128]{2,1,0:T(8,128)}, u32[]{:S(2)}) copy-start(f32[4,256,128]{2,1,0:T(8,128)} %param.13) | copy-start | bytes 1572868
  3.9 1.1 %copy-start.4 = (f32[4,128,256]{2,1,0:T(8,128)}, f32[4,128,256]{2,1,0:T(8,128)S(1)}, u32[]{:S(2)}) copy-start(f32[4,128,256]{2,1,0:T(8,128)S(1)} %fusion.219) | copy-start | bytes 1572868
  3.9 1.3 %copy-start.9 = (f32[3,256,256]{2,1,0:T(8,128)S(1)}, f32[3,256,256]{2,1,0:T(8,128)}, u32[]{:S(2)}) copy-start(f32[3,256,256]{2,1,0:T(8,128)} %param.14) | copy-start | bytes 2359300
  5.0 1.2 %copy-start.7 = (f32[3,256,256]{2,1,0:T(8,128)S(1)}, f32[3,256,256]{2,1,0:T(8,128)}, u32[]{:S(2)}) copy-start(f32[3,256,256]{2,1,0:T(8,128)} %param.15) | copy-start | bytes 2359300
  6.2 1.0 %copy-start.13 = (f32[3,256,128]{2,1,0:T(8,128)S(1)}, f32[3,256,128]{2,1,0:T(8,128)}, u32[]{:S(2)}) copy-start(f32[3,256,128]{2,1,0:T(8,128)} %param.16) | copy-start | bytes 1179652
  7.2 4.1 %copy-start.2 = (f32[4,256,256]{2,1,0:T(8,128)S(1)}, f32[4,256,256]{2,1,0:T(8,128)}, u32[]{:S(2)}) copy-start(f32[4,256,256]{2,1,0:T(8,128)} %param.17) | copy-start | bytes 3145732
  7.8 4.7 %copy-start.1 = (f32[4,256,256]{2,1,0:T(8,128)S(1)}, f32[4,256,256]{2,1,0:T(8,128)}, u32[]{:S(2)}) copy-start(f32[4,256,256]{2,1,0:T(8,128)} %param.18) | copy-start | bytes 3145732
  9.6 1.7 %collective-permute-start = (f32[1,128,64]{1,2,0:T(8,128)}, f32[1,128,64]{1,2,0:T(8,128)}, u32[]{:S(2)}, u32[]{:S(2)}) collective-permute-start(f32[1,128,64]{1,2,0:T(8,128)} %get-tuple-element.5), channel_id=1, source_target_pairs={{0,1},{1,0},{2,3},{3,2},{4,5},{5,4},{6,7},{7,6},{8,9},{9,8},{10,11... | collective-permute-start | bytes 98312 | tf_op jit(solution)/shard_map/ppermute | solution.py:12
  10.1 5.9 %collective-permute-start.4 = (f32[1,128,64]{1,2,0:T(8,128)}, f32[1,128,64]{1,2,0:T(8,128)}, u32[]{:S(2)}, u32[]{:S(2)}) collective-permute-start(f32[1,128,64]{1,2,0:T(8,128)} %get-tuple-element.8), channel_id=1, source_target_pairs={{0,1},{1,0},{2,3},{3,2},{4,5},{5,4},{6,7},{7,6},{8,9},{9,8},{10,11... | collective-permute-start | bytes 98312 | tf_op jit(solution)/shard_map/ppermute | solution.py:12
  10.1 2.8 %copy-start.3 = (f32[4,256,128]{2,1,0:T(8,128)S(1)}, f32[4,256,128]{2,1,0:T(8,128)}, u32[]{:S(2)}) copy-start(f32[4,256,128]{2,1,0:T(8,128)} %param.19) | copy-start | bytes 1572868
  12.9 3.2 %copy-start.15 = (f32[128,64]{0,1:T(8,128)S(1)}, f32[128,64]{0,1:T(8,128)}, u32[]{:S(2)}) copy-start(f32[128,64]{0,1:T(8,128)} %get-tuple-element.7) | copy-start | bytes 98308
  13.1 5.2 %collective-permute-start.1 = (f32[1,128,64]{1,2,0:T(8,128)S(1)}, f32[1,128,64]{1,2,0:T(8,128)S(1)}, u32[]{:S(2)}, u32[]{:S(2)}) collective-permute-start(f32[1,128,64]{1,2,0:T(8,128)S(1)} %bitcast.270), channel_id=1, source_target_pairs={{0,2},{1,3},{2,0},{3,1},{4,6},{5,7},{6,4},{7,5},{8,10},{9,11},{10,... | collective-permute-start | bytes 98312 | tf_op jit(solution)/shard_map/ppermute | solution.py:12
  17.8 4.0 %collective-permute-start.5 = (f32[1,128,64]{1,2,0:T(8,128)S(1)}, f32[1,128,64]{1,2,0:T(8,128)S(1)}, u32[]{:S(2)}, u32[]{:S(2)}) collective-permute-start(f32[1,128,64]{1,2,0:T(8,128)S(1)} %bitcast.272), channel_id=1, source_target_pairs={{0,2},{1,3},{2,0},{3,1},{4,6},{5,7},{6,4},{7,5},{8,10},{9,11},{10,... | collective-permute-start | bytes 98312 | tf_op jit(solution)/shard_map/ppermute | solution.py:12
  19.3 5.1 %collective-permute-start.2 = (f32[1,128,64]{1,2,0:T(8,128)S(1)}, f32[1,128,64]{1,2,0:T(8,128)S(1)}, u32[]{:S(2)}, u32[]{:S(2)}) collective-permute-start(f32[1,128,64]{1,2,0:T(8,128)S(1)} %bitcast.274), channel_id=1, source_target_pairs={{0,4},{1,5},{2,6},{3,7},{4,0},{5,1},{6,2},{7,3},{8,12},{9,13},{10,... | collective-permute-start | bytes 98312 | tf_op jit(solution)/shard_map/ppermute | solution.py:12
  22.8 5.3 %collective-permute-start.6 = (f32[1,128,64]{1,2,0:T(8,128)S(1)}, f32[1,128,64]{1,2,0:T(8,128)S(1)}, u32[]{:S(2)}, u32[]{:S(2)}) collective-permute-start(f32[1,128,64]{1,2,0:T(8,128)S(1)} %bitcast.276), channel_id=1, source_target_pairs={{0,4},{1,5},{2,6},{3,7},{4,0},{5,1},{6,2},{7,3},{8,12},{9,13},{10,... | collective-permute-start | bytes 98312 | tf_op jit(solution)/shard_map/ppermute | solution.py:12
  25.4 5.2 %collective-permute-start.3 = (f32[1,128,64]{1,2,0:T(8,128)S(1)}, f32[1,128,64]{1,2,0:T(8,128)S(1)}, u32[]{:S(2)}, u32[]{:S(2)}) collective-permute-start(f32[1,128,64]{1,2,0:T(8,128)S(1)} %bitcast.278), channel_id=1, source_target_pairs={{0,8},{1,9},{2,10},{3,11},{4,12},{5,13},{6,14},{7,15},{8,0},{9,1},... | collective-permute-start | bytes 98312 | tf_op jit(solution)/shard_map/ppermute | solution.py:12
  29.0 5.2 %collective-permute-start.7 = (f32[1,128,64]{1,2,0:T(8,128)S(1)}, f32[1,128,64]{1,2,0:T(8,128)S(1)}, u32[]{:S(2)}, u32[]{:S(2)}) collective-permute-start(f32[1,128,64]{1,2,0:T(8,128)S(1)} %bitcast.268), channel_id=1, source_target_pairs={{0,8},{1,9},{2,10},{3,11},{4,12},{5,13},{6,14},{7,15},{8,0},{9,1},... | collective-permute-start | bytes 98312 | tf_op jit(solution)/shard_map/ppermute | solution.py:12
  36.9 1.6 %copy-start.8 = (f32[3,256,256]{2,1,0:T(8,128)S(1)}, f32[3,256,256]{2,1,0:T(8,128)}, u32[]{:S(2)}) copy-start(f32[3,256,256]{2,1,0:T(8,128)} %param.15) | copy-start | bytes 2359300
  37.2 1.0 %copy-start.14 = (f32[3,256,128]{2,1,0:T(8,128)S(1)}, f32[3,256,128]{2,1,0:T(8,128)}, u32[]{:S(2)}) copy-start(f32[3,256,128]{2,1,0:T(8,128)} %param.16) | copy-start | bytes 1179652
  37.6 1.3 %copy-start.10 = (f32[3,256,256]{2,1,0:T(8,128)S(1)}, f32[3,256,256]{2,1,0:T(8,128)}, u32[]{:S(2)}) copy-start(f32[3,256,256]{2,1,0:T(8,128)} %param.14) | copy-start | bytes 2359300
  40.8 1.0 %copy-start.12 = (f32[4,256,128]{2,1,0:T(8,128)S(1)}, f32[4,256,128]{2,1,0:T(8,128)}, u32[]{:S(2)}) copy-start(f32[4,256,128]{2,1,0:T(8,128)} %param.13) | copy-start | bytes 1572868
  41.8 1.0 %copy-start.5 = (f32[4,128,256]{2,1,0:T(8,128)S(1)}, f32[4,128,256]{2,1,0:T(8,128)}, u32[]{:S(2)}) copy-start(f32[4,128,256]{2,1,0:T(8,128)} %copy-done.4) | copy-start | bytes 1572868
  42.9 1.2 %copy-start.6 = (f32[4,256,256]{2,1,0:T(8,128)S(1)}, f32[4,256,256]{2,1,0:T(8,128)}, u32[]{:S(2)}) copy-start(f32[4,256,256]{2,1,0:T(8,128)} %param.11) | copy-start | bytes 3145732
where the time goes:
time: 46.4 us; the launch traced here: 45.8 us
  matrix products  27.3 us (59%)
  starting transfers between devices  11.3 us (24%)
  local copies, waits for them, and re-layouts  4.45 us (10%)
  waiting for transfers between devices  2.34 us (5%)
    dot_general x40, matrix products, batched(): return jnp.einsum('nij,njr->nir', mats, vecs, precision=HIGH)  21.1 us
    ppermute x8, starting transfers between devices, swapped(): return lax.ppermute(value, axis, pairs)  11.3 us
    dot_general x18, matrix products, batched_t(): return jnp.einsum('nji,njr->nir', mats, vecs, precision=HIGH)  6.25 us
    unnamed x32, local copies, waits for them, and re-layouts  2.57 us
    ppermute x8, waiting for transfers between devices, swapped(): return lax.ppermute(value, axis, pairs)  2.34 us
    dot_general x3, local copies, waits for them, and re-layouts, batched_t(): return jnp.einsum('nji,njr->nir', mats, vecs, precision=HIGH)  1.22 us
  transfers between devices with their start and end apart: 8, of which 4 were waited for; matrix products, arithmetic and copies ran while one was open for 24% of the time, Pallas kernels for 0%

commit v1 on v0

v1 whole, which is shorter than its diff:
```python
import functools

import jax
import jax.numpy as jnp
from jax import lax
from jax.experimental import pallas as pl
from jax.experimental.pallas import tpu as pltpu
from jax.sharding import PartitionSpec as P

F32 = jnp.float32
BF16 = jnp.bfloat16


def split(x):
    hi = x.astype(BF16)
    return hi, (x - hi.astype(F32)).astype(BF16)


def mul(a, b):
    left = jnp.concatenate([a[0], a[0], a[1]], axis=1)
    right = jnp.concatenate([b[0], b[1], b[0]], axis=0)
    return jnp.dot(left, right, preferred_element_type=F32)


def rows(pair, start, count):
    return pair[0][start : start + count], pair[1][start : start + count]


def beside(*pairs):
    return (
        jnp.concatenate([p[0] for p in pairs], axis=1),
        jnp.concatenate([p[1] for p in pairs], axis=1),
    )


def call(kernel, outs, ins, scratch=(), hbm_ins=()):
    specs = [
        pl.BlockSpec(memory_space=pltpu.HBM if i in hbm_ins else pltpu.VMEM)
        for i in range(len(ins))
    ]
    return pl.pallas_call(
        kernel,
        out_shape=[jax.ShapeDtypeStruct(s, d) for s, d in outs],
        in_specs=specs,
        out_specs=[pl.BlockSpec(memory_space=pltpu.VMEM) for _ in outs],
        scratch_shapes=list(scratch),
        compiler_params=pltpu.CompilerParams(vmem_limit_bytes=24 << 20),
    )(*[pltpu.with_memory_space_constraint(x, pltpu.HBM) if i in hbm_ins else x for i, x in enumerate(ins)])


def up_kernel(
    rhs, lq, le, lw, nq, ne, nw, tq, te, tw,
    c0, yl, yn, lqv, lev, lwv, nqv, nev, nwv, tqv, tev, twv,
    rhsv, sems,
):
    leaves = rhs.shape[0]
    nodes = nq.shape[0]
    width = lw.shape[2]
    copies = {}

    def start(name, src, dst):
        copy = pltpu.make_async_copy(src, dst, sems.at[len(copies)])
        copy.start()
        copies[name] = copy

    start("b", rhs, rhsv)
    for i in range(leaves):
        start(("q", i), lq.at[i], lqv.at[i])
    for i in range(leaves):
        start(("e", i), le.at[i], lev.at[i])
    start("w", lw, lwv)
    start("nq", nq, nqv)
    start("ne", ne, nev)
    start("nw", nw, nwv)
    start("tq", tq, tqv)
    start("te", te, tev)
    start("tw", tw, twv)

    copies["b"].wait()
    mid = []
    for i in range(leaves):
        copies["q", i].wait()
        mid.append(mul(split(lqv[i]), split(rhsv[i])))
    vals = []
    for i in range(leaves):
        copies["e", i].wait()
        y = mul(split(lev[i]), split(mid[i]))
        yl[i] = y
        vals.append(y)
    copies["w"].wait()
    reduced = [mul(split(lwv[i].T), split(vals[i])) for i in range(leaves)]
    copies["nq"].wait()
    copies["ne"].wait()
    copies["nw"].wait()
    offset = 0
    while len(reduced) > 1:
        count = len(reduced) // 2
        b = [jnp.concatenate(reduced[2 * j : 2 * j + 2], axis=0) for j in range(count)]
        t = [mul(split(nqv[offset + j]), split(b[j])) for j in range(count)]
        y = [mul(split(nev[offset + j]), split(t[j])) for j in range(count)]
        for j in range(count):
            yn[offset + j] = y[j]
        reduced = [mul(split(nwv[offset + j].T), split(y[j])) for j in range(count)]
        offset += count
    c0[...] = reduced[0]
    copies["tq"].wait()
    copies["te"].wait()
    copies["tw"].wait()


def side_of(level):
    position = lax.axis_index("leaf")
    return lax.rem(position // 2 ** (level - 1), 2)


def level_kernel(level, last, first, tq, te, tw, *refs):
    if first:
        t_in, outs = None, refs
    else:
        t_in, outs = refs[0], refs[1:]
    width = tw.shape[2]
    side = side_of(level)
    start = pl.multiple_of(side * width, width)
    q = split(tq[level - 1])
    if last:
        e_rows = split(te[level - 1, pl.ds(start, width), :])
        eq = mul(e_rows, q)
        if not first:
            eq = mul(split(t_in[...]), split(eq))
        outs[0][...] = eq
        return
    w = tw[level - 1]
    x = split(mul(split(te[level - 1]), beside(q, split(w))))
    q_half = tq[level - 1, :, pl.ds(start, width)]
    y = mul(split(jnp.concatenate([w.T, q_half.T], axis=0)), x)
    outs[0][:width] = y[:width, : 2 * width]
    low = y[width:]
    if not first:
        low = mul(split(t_in[...]), split(low))
    outs[0][width:] = low[:, : 2 * width]
    outs[1][...] = -low[:, 2 * width :]


def step_kernel(level, last, first, mat, own, other, *refs):
    if first:
        k_in, outs = None, refs
    else:
        k_in, outs = refs[0], refs[1:]
    width = own.shape[0]
    right = side_of(level) == 1
    a, b = own[...], other[...]
    both = jnp.concatenate(
        [jnp.where(right, b, a), jnp.where(right, a, b)], axis=0
    )
    out = mul(split(mat[...]), split(both))
    k = out if last else out[width:]
    if not first:
        k = k + k_in[...]
    if not last:
        outs[0][...] = out[:width]
    outs[-1][...] = k


def descent_kernel(q, e, w, y, after, out):
    for i in range(q.shape[0]):
        ew = mul(split(e[i]), split(w[i]))
        out[i] = mul(split(q[i].T), beside(split(y[i]), split(ew)))


def compose_kernel(nq, ne, nw, yn, leaf_maps, after, const, coef):
    width = nw.shape[2]
    nodes = nq.shape[0]
    maps = []
    for i in range(nodes):
        ew = mul(split(ne[i]), split(nw[i]))
        maps.append(mul(split(nq[i].T), beside(split(yn[i]), split(ew))))
    cols = yn.shape[2]
    top = maps[-1]
    parent = [jnp.concatenate([top[:, :cols], -top[:, cols:]], axis=1)]

    def below(vg, block):
        moved = mul(split(vg[:, cols:]), split(block))
        return jnp.concatenate([vg[:, :cols] - moved[:, :cols], -moved[:, cols:]], axis=1)

    count, offset = 1, nodes - 1
    while offset > 0:
        count *= 2
        offset -= count
        parent = [
            below(maps[offset + j], parent[j // 2][j % 2 * width : (j % 2 + 1) * width])
            for j in range(count)
        ]
    for i in range(leaf_maps.shape[0]):
        full = below(leaf_maps[i], parent[i // 2][i % 2 * width : (i % 2 + 1) * width])
        const[i] = full[:, :cols]
        coef[i] = full[:, cols:]


def final_kernel(level, mat, own, other, k, const, coef, out):
    width = own.shape[0]
    right = side_of(level) == 1
    a, b = own[...], other[...]
    both = jnp.concatenate(
        [jnp.where(right, b, a), jnp.where(right, a, b)], axis=0
    )
    g = split(mul(split(mat[...]), split(both)) + k[...])
    for i in range(out.shape[0]):
        out[i] = const[i] + mul(split(coef[i]), g)


def swapped(value, apart):
    pairs = [(i, i ^ 2**apart) for i in range(lax.axis_size("leaf"))]
    return lax.ppermute(value, "leaf", pairs)


def body(rhs, leaf_q, leaf_e, leaf_w, node_q, node_e, node_w, top_q, top_e, top_w):
    leaves, size, cols = rhs.shape
    nodes = node_q.shape[0]
    width = leaf_w.shape[2]
    levels = lax.axis_size("leaf").bit_length() - 1
    sq = (size, size)
    copies_of = [(a.shape, F32) for a in (leaf_q, leaf_e, leaf_w, node_q, node_e, node_w, top_q, top_e, top_w)]
    res = call(
        up_kernel,
        [((width, cols), F32), ((leaves, size, cols), F32), ((nodes, size, cols), F32)] + copies_of,
        [rhs, leaf_q, leaf_e, leaf_w, node_q, node_e, node_w, top_q, top_e, top_w],
        scratch=[pltpu.VMEM(rhs.shape, F32), pltpu.SemaphoreType.DMA((2 * leaves + 8,))],
        hbm_ins=range(10),
    )
    block, yl, yn, lq, le, lw, nq, ne, nw, tq, te, tw = res

    trans = []
    k = []
    leaf_maps = call(
        descent_kernel, [((leaves, size, cols + width), F32)], [lq, le, lw, yl, block]
    )[0]
    const, coef = call(
        compose_kernel,
        [((leaves, size, cols), F32), ((leaves, size, width), F32)],
        [nq, ne, nw, yn, leaf_maps, block],
    )
    for level in range(1, levels + 1):
        first, last = level == 1, level == levels
        other = swapped(block, level - 1)
        outs = [((width, size), F32)] if last else [((2 * width, size), F32), ((width, width), F32)]
        made = call(
            functools.partial(level_kernel, level, last, first), outs, [tq, te, tw] + trans
        )
        trans = list(made[1:])
        if last:
            return call(
                functools.partial(final_kernel, level),
                [((leaves, size, cols), F32)],
                [made[0], block, other, k[0], const, coef],
            )[0]
        block, k_new = call(
            functools.partial(step_kernel, level, last, first),
            [((width, cols), F32), ((width, cols), F32)],
            [made[0], block, other] + k,
        )
        k = [k_new]


def solution(mesh):
    spec = P(("freq", "leaf"), None, None)
    return jax.shard_map(body, mesh=mesh, in_specs=(spec,) * 10, out_specs=spec, check_vma=False)
```

time: 46.4 us -> 25.6 us (0.55)
  matrix products: 27.3 us -> 0 us
  Pallas kernels: 0 us -> 13.7 us
  local copies, waits for them, and re-layouts: 4.45 us -> 0 us
  starting transfers between devices: 11.3 us -> 8.43 us
  waiting for transfers between devices: 2.34 us -> 3.18 us
    dot_general x58 -> x0, matrix products: 27.3 us -> none  [the longest x40 21.1 us: batched(): return jnp.einsum('nij,njr->nir', mats, vecs, precision=HIGH)]
    pallas_call x0 -> x11, Pallas kernels: none -> 13.7 us  [call(): pl.pallas_call(kernel, out_shape=[jax.ShapeDtypeStruct(s, d) for s, d in...]
    ppermute x8 -> x4, starting transfers between devices: 11.3 us -> 8.43 us  [swapped(): return lax.ppermute(value, 'leaf', pairs)]
    unnamed x32 -> x0, local copies, waits for them, and re-layouts: 2.57 us -> none
    dot_general x3 -> x0, local copies, waits for them, and re-layouts: 1.22 us -> none  [batched_t(): return jnp.einsum('nji,njr->nir', mats, vecs, precision=HIGH)]
    ppermute x8 -> x4, waiting for transfers between devices: 2.34 us -> 3.18 us  [swapped(): return lax.ppermute(value, 'leaf', pairs)]
    slice x1 -> x0, local copies, waits for them, and re-layouts: 0.65 us -> none  [body(): first = tree_sweep(reduced[:, :, :half], top_q, top_e, top_w, width)]
  transfers between devices with their start and end apart: 8 -> 4, of which waited for: 4 -> 3; matrix products, arithmetic and copies ran while one was open for 24% -> 0% of each run, Pallas kernels for 0% -> 24%
where the time goes in v1:
time: 25.6 us; the launch traced here: 25.4 us
  Pallas kernels  13.7 us (54%)
  starting transfers between devices  8.43 us (33%)
  waiting for transfers between devices  3.18 us (12%)
    pallas_call x11, Pallas kernels, call(): pl.pallas_call(kernel, out_shape=[jax.ShapeDtypeStruct(s, d) for s, d in...  13.7 us
    ppermute x4, starting transfers between devices, swapped(): return lax.ppermute(value, 'leaf', pairs)  8.43 us
    ppermute x4, waiting for transfers between devices, swapped(): return lax.ppermute(value, 'leaf', pairs)  3.18 us
  transfers between devices with their start and end apart: 4, of which 3 were waited for; matrix products, arithmetic and copies ran while one was open for 0% of the time, Pallas kernels for 24%

profile of v1, /device:TPU:0, one launch (start us, length us, event | category | flops | bytes accessed | tf_op | source)
XLA Modules:
  0.0 25.4 jit_solution(5105234464914436340)
XLA Ops:
  0.0 5.6 %shard_map.100 = (f32[128,128]{1,0:T(8,128)S(1)}, f32[4,256,128]{2,1,0:T(8,128)S(1)}, f32[3,256,128]{2,1,0:T(8,128)S(1)}, f32[4,256,256]{2,1,0:T(8,128)S(1)}, f3...) custom-call(f32[4,256,128]{2,1,0:T(8,128)} %rhs.1, ...), custom_call_target="tpu_custom_call" | custom-call | tf_op jit(solution)/shard_map/pallas_call | solution.py:41
  5.6 0.6 %collective-permute-start = (f32[128,128]{1,0:T(8,128)S(1)}, f32[128,128]{1,0:T(8,128)S(1)}, u32[]{:S(2)}, u32[]{:S(2)}) collective-permute-start(f32[128,128]{1,0:T(8,128)S(1)} %get-tuple-element.40.own.after), channel_id=1, source_target_pairs={{0,1},{1,0},{2,3},{3,2},{4,5},{5,4},{6,7},{7,6},{8,9},{9,8},{10,11... | collective-permute-start | bytes 196616 | tf_op jit(solution)/shard_map/ppermute | solution.py:213
  6.1 0.7 %shard_map.101 = (f32[256,256]{1,0:T(8,128)S(1)}, f32[128,128]{1,0:T(8,128)S(1)}) custom-call(f32[4,256,256]{2,1,0:T(8,128)S(1)} %get-tuple-element.31.tq, f32[4,256,256]{2,1,0:T(8,128)S(1)} %get-tuple-element.32.te, f32[4,256,128]{2,1,0:T(8,128)S(1)} %get-tuple-element.33.tw), custom_call_target="tpu_custom_call" | custom-call | tf_op jit(solution)/shard_map/pallas_call | solution.py:41
  6.8 0.2 collective-permute-done.other
  7.0 0.3 shard_map.105
  7.3 2.9 %collective-permute-start.1 = (f32[128,128]{1,0:T(8,128)S(1)}, f32[128,128]{1,0:T(8,128)S(1)}, u32[]{:S(2)}, u32[]{:S(2)}) collective-permute-start(f32[128,128]{1,0:T(8,128)S(1)} %get-tuple-element.41.own), channel_id=1, source_target_pairs={{0,2},{1,3},{2,0},{3,1},{4,6},{5,7},{6,4},{7,5},{8,10},{9,11},{10,... | collective-permute-start | bytes 196616 | tf_op jit(solution)/shard_map/ppermute | solution.py:213
  10.2 0.9 %shard_map.102 = (f32[256,256]{1,0:T(8,128)S(1)}, f32[128,128]{1,0:T(8,128)S(1)}) custom-call(f32[4,256,256]{2,1,0:T(8,128)S(1)} %get-tuple-element.31.tq, f32[4,256,256]{2,1,0:T(8,128)S(1)} %get-tuple-element.32.te, f32[4,256,128]{2,1,0:T(8,128)S(1)} %get-tuple-element.33.tw, f32[128,128]{1,0:T(8,128)S(1)} %get-tuple-element.34.refs_0_), custom_call_target="tpu_custom_call" | custom-call | tf_op jit(solution)/shard_map/pallas_call | solution.py:41
  11.1 1.5 %collective-permute-done.1.other = f32[128,128]{1,0:T(8,128)S(1)} collective-permute-done((f32[128,128]{1,0:T(8,128)S(1)}, f32[128,128]{1,0:T(8,128)S(1)}, u32[]{:S(2)}, u32[]{:S(2)}) %collective-permute-start.1) | collective-permute-done | bytes 65568 | tf_op jit(solution)/shard_map/ppermute | solution.py:213
  12.6 0.3 %shard_map.106 = (f32[128,128]{1,0:T(8,128)S(1)}, f32[128,128]{1,0:T(8,128)S(1)}) custom-call(f32[256,256]{1,0:T(8,128)S(1)} %get-tuple-element.38.mat, f32[128,128]{1,0:T(8,128)S(1)} %get-tuple-element.41.own, f32[128,128]{1,0:T(8,128)S(1)} %collective-permute-done.1.other, f32[128,128]{1,0:T(8,128)S(1)} %get-tuple-element.42.refs_0_), custom_call_target="tpu_custom_call" | custom-call | tf_op jit(solution)/shard_map/pallas_call | solution.py:41
  12.9 2.0 %collective-permute-start.2 = (f32[128,128]{1,0:T(8,128)S(1)}, f32[128,128]{1,0:T(8,128)S(1)}, u32[]{:S(2)}, u32[]{:S(2)}) collective-permute-start(f32[128,128]{1,0:T(8,128)S(1)} %get-tuple-element.43.own), channel_id=1, source_target_pairs={{0,4},{1,5},{2,6},{3,7},{4,0},{5,1},{6,2},{7,3},{8,12},{9,13},{10,... | collective-permute-start | bytes 196616 | tf_op jit(solution)/shard_map/ppermute | solution.py:213
  14.9 0.9 %shard_map.103 = (f32[256,256]{1,0:T(8,128)S(1)}, f32[128,128]{1,0:T(8,128)S(1)}) custom-call(f32[4,256,256]{2,1,0:T(8,128)S(1)} %get-tuple-element.31.tq, f32[4,256,256]{2,1,0:T(8,128)S(1)} %get-tuple-element.32.te, f32[4,256,128]{2,1,0:T(8,128)S(1)} %get-tuple-element.33.tw, f32[128,128]{1,0:T(8,128)S(1)} %get-tuple-element.35.refs_0_), custom_call_target="tpu_custom_call" | custom-call | tf_op jit(solution)/shard_map/pallas_call | solution.py:41
  15.8 1.5 %collective-permute-done.2.other = f32[128,128]{1,0:T(8,128)S(1)} collective-permute-done((f32[128,128]{1,0:T(8,128)S(1)}, f32[128,128]{1,0:T(8,128)S(1)}, u32[]{:S(2)}, u32[]{:S(2)}) %collective-permute-start.2) | collective-permute-done | bytes 65568 | tf_op jit(solution)/shard_map/ppermute | solution.py:213
  17.2 0.3 %shard_map.107 = (f32[128,128]{1,0:T(8,128)S(1)}, f32[128,128]{1,0:T(8,128)S(1)}) custom-call(f32[256,256]{1,0:T(8,128)S(1)} %get-tuple-element.37.mat, f32[128,128]{1,0:T(8,128)S(1)} %get-tuple-element.43.own, f32[128,128]{1,0:T(8,128)S(1)} %collective-permute-done.2.other, f32[128,128]{1,0:T(8,128)S(1)} %get-tuple-element.44.refs_0_), custom_call_target="tpu_custom_call" | custom-call | tf_op jit(solution)/shard_map/pallas_call | solution.py:41
  17.5 3.0 %collective-permute-start.3 = (f32[128,128]{1,0:T(8,128)S(1)}, f32[128,128]{1,0:T(8,128)S(1)}, u32[]{:S(2)}, u32[]{:S(2)}) collective-permute-start(f32[128,128]{1,0:T(8,128)S(1)} %get-tuple-element.45.own), channel_id=1, source_target_pairs={{0,8},{1,9},{2,10},{3,11},{4,12},{5,13},{6,14},{7,15},{8,0},{9,1},... | collective-permute-start | bytes 196616 | tf_op jit(solution)/shard_map/ppermute | solution.py:213
  20.5 0.4 %shard_map.104.mat = f32[128,256]{1,0:T(8,128)S(1)} custom-call(f32[4,256,256]{2,1,0:T(8,128)S(1)} %get-tuple-element.31.tq, f32[4,256,256]{2,1,0:T(8,128)S(1)} %get-tuple-element.32.te, f32[4,256,128]{2,1,0:T(8,128)S(1)} %get-tuple-element.33.tw, f32[128,128]{1,0:T(8,128)S(1)} %get-tuple-element.36.refs_0_), custom_call_target="tpu_custom_call" | custom-call | tf_op jit(solution)/shard_map/pallas_call | solution.py:41
  20.9 1.4 %shard_map.108.leaf_maps = f32[4,256,256]{2,1,0:T(8,128)S(1)} custom-call(f32[4,256,256]{2,1,0:T(8,128)S(1)} %get-tuple-element.51.q, f32[4,256,256]{2,1,0:T(8,128)S(1)} %get-tuple-element.52.e, f32[4,256,128]{2,1,0:T(8,128)S(1)} %get-tuple-element.53.w, f32[4,256,128]{2,1,0:T(8,128)S(1)} %get-tuple-element.54.y, f32[128,128]{1,0:T(8,128)S(1)} %get-tuple-element.40.own.after), custom_call_target="tpu_custom_call" | custom-call | tf_op jit(solution)/shard_map/pallas_call | solution.py:41
  22.4 1.7 %shard_map.109 = (f32[4,256,128]{2,1,0:T(8,128)S(1)}, f32[4,256,128]{2,1,0:T(8,128)S(1)}) custom-call(f32[3,256,256]{2,1,0:T(8,128)S(1)} %get-tuple-element.47.nq, f32[3,256,256]{2,1,0:T(8,128)S(1)} %get-tuple-element.48.ne, f32[3,256,128]{2,1,0:T(8,128)S(1)} %get-tuple-element.49.nw, f32[3,256,128]{2,1,0:T(8,128)S(1)} %get-tuple-element.50.yn, ...), custom_call_target="tpu_custom_call" | custom-call | tf_op jit(solution)/shard_map/pallas_call | solution.py:41
  24.1 0.0 collective-permute-done.3.other
  24.1 1.4 %shard_map.110 = f32[4,256,128]{2,1,0:T(8,128)} custom-call(f32[128,256]{1,0:T(8,128)S(1)} %shard_map.104.mat, f32[128,128]{1,0:T(8,128)S(1)} %get-tuple-element.45.own, f32[128,128]{1,0:T(8,128)S(1)} %collective-permute-done.3.other, f32[128,128]{1,0:T(8,128)S(1)} %get-tuple-element.46.k, f32[4,256,128]{2,1,0:T(8,128)S(1)} %get-tuple-element.55.const, ...), custom_call_target="tpu_custom_call" | custom-call | tf_op jit(solution)/shard_map/pallas_call | solution.py:41
Async XLA Ops:
  5.6 1.5 %collective-permute-start = (f32[128,128]{1,0:T(8,128)S(1)}, f32[128,128]{1,0:T(8,128)S(1)}, u32[]{:S(2)}, u32[]{:S(2)}) collective-permute-start(f32[128,128]{1,0:T(8,128)S(1)} %get-tuple-element.40.own.after), channel_id=1, source_target_pairs={{0,1},{1,0},{2,3},{3,2},{4,5},{5,4},{6,7},{7,6},{8,9},{9,8},{10,11... | collective-permute-start | bytes 196616 | tf_op jit(solution)/shard_map/ppermute | solution.py:213
  7.3 5.3 %collective-permute-start.1 = (f32[128,128]{1,0:T(8,128)S(1)}, f32[128,128]{1,0:T(8,128)S(1)}, u32[]{:S(2)}, u32[]{:S(2)}) collective-permute-start(f32[128,128]{1,0:T(8,128)S(1)} %get-tuple-element.41.own), channel_id=1, source_target_pairs={{0,2},{1,3},{2,0},{3,1},{4,6},{5,7},{6,4},{7,5},{8,10},{9,11},{10,... | collective-permute-start | bytes 196616 | tf_op jit(solution)/shard_map/ppermute | solution.py:213
  12.9 4.3 %collective-permute-start.2 = (f32[128,128]{1,0:T(8,128)S(1)}, f32[128,128]{1,0:T(8,128)S(1)}, u32[]{:S(2)}, u32[]{:S(2)}) collective-permute-start(f32[128,128]{1,0:T(8,128)S(1)} %get-tuple-element.43.own), channel_id=1, source_target_pairs={{0,4},{1,5},{2,6},{3,7},{4,0},{5,1},{6,2},{7,3},{8,12},{9,13},{10,... | collective-permute-start | bytes 196616 | tf_op jit(solution)/shard_map/ppermute | solution.py:213
  17.5 6.6 %collective-permute-start.3 = (f32[128,128]{1,0:T(8,128)S(1)}, f32[128,128]{1,0:T(8,128)S(1)}, u32[]{:S(2)}, u32[]{:S(2)}) collective-permute-start(f32[128,128]{1,0:T(8,128)S(1)} %get-tuple-element.45.own), channel_id=1, source_target_pairs={{0,8},{1,9},{2,10},{3,11},{4,12},{5,13},{6,14},{7,15},{8,0},{9,1},... | collective-permute-start | bytes 196616 | tf_op jit(solution)/shard_map/ppermute | solution.py:213

commit v2 on v0

v2 whole, which is shorter than its diff:
```python
import functools

import jax
import jax.numpy as jnp
from jax import lax
from jax.experimental import pallas as pl
from jax.experimental.pallas import tpu as pltpu
from jax.sharding import PartitionSpec as P

F32 = jnp.float32
BF16 = jnp.bfloat16


def split(x):
    hi = x.astype(BF16)
    return hi, (x - hi.astype(F32)).astype(BF16)


def dot(a, b, contract=0):
    return lax.dot_general(a, b, (((1,), (contract,)), ((), ())), preferred_element_type=F32)


def mul(a, b):
    left = jnp.concatenate([a[0], a[0], a[1]], axis=1)
    right = jnp.concatenate([b[0], b[1], b[0]], axis=0)
    return dot(left, right)


def mul_narrow(a, b):
    m, n = a[0].shape[0], b[0].shape[1]
    r = dot(jnp.concatenate(a, axis=0), jnp.concatenate(b, axis=1))
    return r[:m, :n] + (r[:m, n:] + r[m:, :n])


def mul_short(a, b):
    m = a[0].shape[0]
    r = dot(jnp.concatenate(a, axis=0), b[0])
    return r[:m] + (r[m:] + dot(a[0], b[1]))


def beside(*pairs):
    return tuple(jnp.concatenate(parts, axis=1) for parts in zip(*pairs))


def call(kernel, outs, ins, scratch=(), hbm_ins=()):
    specs = [
        pl.BlockSpec(memory_space=pltpu.HBM if i in hbm_ins else pltpu.VMEM)
        for i in range(len(ins))
    ]
    ins = [
        pltpu.with_memory_space_constraint(x, pltpu.HBM) if i in hbm_ins else x
        for i, x in enumerate(ins)
    ]
    made = pl.pallas_call(
        kernel,
        out_shape=[jax.ShapeDtypeStruct(s, d) for s, d in outs],
        in_specs=specs,
        out_specs=[pl.BlockSpec(memory_space=pltpu.VMEM) for _ in outs],
        scratch_shapes=list(scratch),
        compiler_params=pltpu.CompilerParams(vmem_limit_bytes=24 << 20),
    )(*ins)
    return list(made)


def side_of(level):
    return lax.rem(lax.axis_index("leaf") // 2 ** (level - 1), 2)


def columns_of(levels):
    return lax.rem(sum(side_of(level) for level in range(1, levels + 1)), 2)


def up_kernel(
    levels, rhs, lq, le, lw, nq, ne, nw, tq, te, tw,
    keep, send, yl, bn, eqn, lqv, lev, lwv, nqv, nev, nwv, tqv, tev, twv,
    rhsv, sems,
):
    leaves, nodes = rhs.shape[0], nq.shape[0]
    copies = []

    def start(src, dst):
        copy = pltpu.make_async_copy(src, dst, sems.at[len(copies)])
        copy.start()
        copies.append(copy)
        return copy

    got_b = start(rhs, rhsv)
    got_q = [start(lq.at[i], lqv.at[i]) for i in range(leaves)]
    got_nq, got_ne = start(nq, nqv), start(ne, nev)
    got_e = [start(le.at[i], lev.at[i]) for i in range(leaves)]
    got_lw, got_nw = start(lw, lwv), start(nw, nwv)
    got_top = [start(tq, tqv), start(te, tev), start(tw, twv)]

    got_b.wait()
    mid, vals = [], []
    for i in range(0, leaves, 2):
        for j in (i, i + 1):
            got_q[j].wait()
        for j in (i, i + 1):
            mid.append(split(mul_narrow(split(lqv[j]), split(rhsv[j]))))
    got_nq.wait()
    got_ne.wait()
    eqs = []
    for i in range(nodes):
        eq = mul(split(nev[i]), split(nqv[i]))
        eqn[i] = eq
        eqs.append(split(eq))
    for i in range(0, leaves, 2):
        for j in (i, i + 1):
            got_e[j].wait()
        for j in (i, i + 1):
            y = mul_narrow(split(lev[j]), mid[j])
            yl[j] = y
            vals.append(split(y))
    got_lw.wait()
    got_nw.wait()
    maps = [split(mul(split(nwv[i].T), eqs[i])) for i in range(nodes)]
    reduced = [mul_narrow(split(lwv[i].T), vals[i]) for i in range(leaves)]
    offset = 0
    while len(reduced) > 1:
        count = len(reduced) // 2
        b = [jnp.concatenate(reduced[2 * j : 2 * j + 2], axis=0) for j in range(count)]
        for j in range(count):
            bn[offset + j] = b[j]
        reduced = [mul_narrow(maps[offset + j], split(b[j])) for j in range(count)]
        offset += count
    c = reduced[0].T
    half = c.shape[0] // 2
    low = columns_of(levels) == 0
    keep[...] = jnp.where(low, c[:half], c[half:])
    send[...] = jnp.where(low, c[half:], c[:half])
    for copy in got_top:
        copy.wait()


def level_kernel(level, levels, tq, te, tw, *refs):
    first, last = level == 1, level == levels
    outs = refs if first else refs[1:]
    width = tw.shape[2]
    half = pl.ds(pl.multiple_of(side_of(level) * width, width), width)
    at = level - 1
    if last:
        c = mul(split(te[at, half, :]), split(tq[at])).T
        if not first:
            c = mul(split(c), split(refs[0][...]))
        outs[0][...], outs[1][...] = split(c)
        return
    e, w = split(te[at]), split(tw[at])
    x = mul(e, split(tq[at]))
    z = mul_narrow(e, w)
    if first:
        q = split(tq[at])
        outs[0][...], outs[1][...] = split(mul(split(x.T), beside(w, q)))
        outs[2][...] = -mul(split(z.T), q)
        return
    q = split(tq[at, :, half])
    both = mul(split(x.T), beside(w, q))
    g = mul_narrow(split(z.T), q)
    low = mul(split(jnp.concatenate([both[:, width:], g], axis=0)), split(refs[0][...]))
    a = split(both[:, :width])
    tb = split(low[: 2 * width])
    for i in range(2):
        outs[i][:, :width] = a[i]
        outs[i][:, width:] = tb[i]
    outs[2][...] = -low[2 * width :]


def family(level, own, other):
    right = side_of(level) == 1
    a, b = own[...], other[...]
    return jnp.concatenate([jnp.where(right, b, a), jnp.where(right, a, b)], axis=1)


def step_kernel(level, hi, lo, own, other, *refs):
    width = own.shape[1]
    both = split(family(level, own, other))
    out = mul_short(both, (hi[...], lo[...]))
    k = out[:, width:]
    if level > 1:
        k = k + refs[0][...]
    refs[-2][...] = out[:, :width]
    refs[-1][...] = k


def root_kernel(level, hi, lo, own, other, *refs):
    width = own.shape[1]
    x = mul_short(split(family(level, own, other)), (hi[...], lo[...]))
    if level > 1:
        x = x + refs[0][...]
    right = side_of(1) == 1
    refs[-2][...] = jnp.where(right, x[:, width:], x[:, :width])
    refs[-1][...] = jnp.where(right, x[:, :width], x[:, width:])


def leaf_kernel(begin, q, e, w, y, after, out):
    for i in range(out.shape[0]):
        at = begin + i
        ew = mul_narrow(split(e[at]), split(w[at]))
        out[i] = mul(split(q[at].T), beside(split(y[at]), split(ew)))


def node_kernel(q, e, w, b, eq, after, out):
    for i in range(out.shape[0]):
        y = mul_narrow(split(eq[i]), split(b[i]))
        ew = mul_narrow(split(e[i]), split(w[i]))
        out[i] = mul(split(q[i].T), beside(split(y), split(ew)))


def compose_kernel(node_maps, maps_a, maps_b, after, const, coef):
    nodes = node_maps.shape[0]
    half = maps_a.shape[0]
    cols = const.shape[2]
    width = maps_a.shape[2] - cols
    top = node_maps[nodes - 1]
    parent = [jnp.concatenate([top[:, :cols], -top[:, cols:]], axis=1)]

    def below(vg, j):
        block = split(parent[j // 2][j % 2 * width : (j % 2 + 1) * width])
        moved = mul(split(vg[:, cols:]), block)
        return jnp.concatenate([vg[:, :cols] - moved[:, :cols], -moved[:, cols:]], axis=1)

    count, offset = 1, nodes - 1
    while offset > 0:
        count *= 2
        offset -= count
        parent = [below(node_maps[offset + j], j) for j in range(count)]
    for i in range(2 * half):
        full = below(maps_a[i] if i < half else maps_b[i - half], i)
        const[i] = full[:, :cols]
        coef[i] = jnp.concatenate(split(full[:, cols:]), axis=1)


def final_kernel(levels, own, other, const, coef, out):
    low = columns_of(levels) == 0
    a, b = own[...], other[...]
    hi, lo = split(
        jnp.concatenate([jnp.where(low, a, b), jnp.where(low, b, a)], axis=0)
    )
    cols = hi.shape[0]
    g = jnp.concatenate(
        [
            jnp.concatenate([hi, hi], axis=1),
            jnp.concatenate([lo, jnp.zeros_like(lo)], axis=1),
        ],
        axis=0,
    )
    for i in range(out.shape[0]):
        moved = dot(coef[i], g, 1)
        out[i] = const[i] + (moved[:, :cols] + moved[:, cols:])


def swapped(value, mask):
    pairs = [(i, i ^ mask) for i in range(lax.axis_size("leaf"))]
    return lax.ppermute(value, "leaf", pairs)


def body(rhs, leaf_q, leaf_e, leaf_w, node_q, node_e, node_w, top_q, top_e, top_w):
    leaves, size, cols = rhs.shape
    nodes = node_q.shape[0]
    width = leaf_w.shape[2]
    levels = lax.axis_size("leaf").bit_length() - 1
    weights = [leaf_q, leaf_e, leaf_w, node_q, node_e, node_w, top_q, top_e, top_w]
    res = call(
        functools.partial(up_kernel, levels),
        [
            ((cols // 2, width), F32),
            ((cols // 2, width), F32),
            (rhs.shape, F32),
            ((nodes, size, cols), F32),
            (node_q.shape, F32),
        ]
        + [(a.shape, F32) for a in weights],
        [rhs] + weights,
        scratch=[pltpu.VMEM(rhs.shape, F32), pltpu.SemaphoreType.DMA((2 * leaves + 8,))],
        hbm_ins=range(10),
    )
    block, sent, yl, bn, eqn, lq, le, lw, nq, ne, nw, tq, te, tw = res

    half = leaves // 2
    leaf_map = lambda begin, after: call(
        functools.partial(leaf_kernel, begin),
        [((half, size, cols + width), F32)],
        [lq, le, lw, yl, after],
    )
    trans, k, maps, done = [], [], [], []
    for level in range(1, levels + 1):
        last = level == levels
        other = swapped(sent if level == 1 else block, 2 ** (level - 1) | 1)
        wide = 2 * width if last else 3 * width
        outs = [((size, wide), BF16)] * 2 + ([] if last else [((width, size), F32)])
        made = call(
            functools.partial(level_kernel, level, levels), outs, [tq, te, tw] + trans
        )
        trans = list(made[2:])
        done = []
        if level == min(2, levels):
            done += leaf_map(0, block)
        if level == min(3, levels):
            done += leaf_map(half, block)
        maps += done
        if last:
            node_maps = call(
                node_kernel,
                [((nodes, size, cols + width), F32)],
                [nq, ne, nw, bn, eqn, block],
            )
            done += node_maps
        block, k_new = call(
            functools.partial(root_kernel if last else step_kernel, level),
            [((cols // 2, width), F32), ((cols // 2, width if last else size), F32)],
            [made[0], made[1], block, other] + k + done,
        )
        k = [k_new]
    other = swapped(k[0], 1)
    const, coef = call(
        compose_kernel,
        [((leaves, size, cols), F32), ((leaves, size, 2 * width), BF16)],
        node_maps + maps + [block],
    )
    return call(
        functools.partial(final_kernel, levels),
        [((leaves, size, cols), F32)],
        [block, other, const, coef],
    )[0]


def solution(mesh):
    spec = P(("freq", "leaf"), None, None)
    return jax.shard_map(body, mesh=mesh, in_specs=(spec,) * 10, out_specs=spec, check_vma=False)
```

time: 46.4 us -> 21.7 us (0.47)
  matrix products: 27.3 us -> 0 us
  Pallas kernels: 0 us -> 13.4 us
  local copies, waits for them, and re-layouts: 4.45 us -> 0 us
  starting transfers between devices: 11.3 us -> 7.75 us
  waiting for transfers between devices: 2.34 us -> 0.23 us
    dot_general x58 -> x0, matrix products: 27.3 us -> none  [the longest x40 21.1 us: batched(): return jnp.einsum('nij,njr->nir', mats, vecs, precision=HIGH)]
    pallas_call x0 -> x14, Pallas kernels: none -> 13.4 us  [call(): pl.pallas_call(kernel, out_shape=[jax.ShapeDtypeStruct(s, d) for s, d in...]
    ppermute x8 -> x5, starting transfers between devices: 11.3 us -> 7.75 us  [swapped(): return lax.ppermute(value, 'leaf', pairs)]
    unnamed x32 -> x0, local copies, waits for them, and re-layouts: 2.57 us -> none
    ppermute x8 -> x5, waiting for transfers between devices: 2.34 us -> 0.23 us  [swapped(): return lax.ppermute(value, 'leaf', pairs)]
    dot_general x3 -> x0, local copies, waits for them, and re-layouts: 1.22 us -> none  [batched_t(): return jnp.einsum('nji,njr->nir', mats, vecs, precision=HIGH)]
    slice x1 -> x0, local copies, waits for them, and re-layouts: 0.65 us -> none  [body(): first = tree_sweep(reduced[:, :, :half], top_q, top_e, top_w, width)]
  transfers between devices with their start and end apart: 8 -> 5, of which waited for: 4 -> 1; matrix products, arithmetic and copies ran while one was open for 24% -> 0% of each run, Pallas kernels for 0% -> 33%
where the time goes in v2:
time: 21.7 us; the launch traced here: 21.5 us
  Pallas kernels  13.4 us (62%)
  starting transfers between devices  7.75 us (36%)
  waiting for transfers between devices  0.23 us (1%)
    pallas_call x14, Pallas kernels, call(): pl.pallas_call(kernel, out_shape=[jax.ShapeDtypeStruct(s, d) for s, d in...  13.4 us
    ppermute x5, starting transfers between devices, swapped(): return lax.ppermute(value, 'leaf', pairs)  7.75 us
  transfers between devices with their start and end apart: 5, of which 1 were waited for; matrix products, arithmetic and copies ran while one was open for 0% of the time, Pallas kernels for 33%

profile of v2, /device:TPU:0, one launch (start us, length us, event | category | flops | bytes accessed | tf_op | source)
XLA Modules:
  0.0 21.5 jit_solution(14244745363817050829)
XLA Ops:
  0.0 4.3 %shard_map.100 = (f32[64,128]{1,0:T(8,128)S(1)}, f32[64,128]{1,0:T(8,128)S(1)}, f32[4,256,128]{2,1,0:T(8,128)S(1)}, f32[3,256,128]{2,1,0:T(8,128)S(1)}, f32[3,25...) custom-call(f32[4,256,128]{2,1,0:T(8,128)} %rhs.1, ...), custom_call_target="tpu_custom_call" | custom-call | tf_op jit(solution)/shard_map/pallas_call | solution.py:54
  4.3 0.6 %collective-permute-start = (f32[64,128]{1,0:T(8,128)S(1)}, f32[64,128]{1,0:T(8,128)S(1)}, u32[]{:S(2)}, u32[]{:S(2)}) collective-permute-start(f32[64,128]{1,0:T(8,128)S(1)} %get-tuple-element.55), channel_id=1, source_target_pairs={{0,1},{1,0},{2,3},{3,2},{4,5},{5,4},{6,7},{7,6},{8,9},{9,8},{10,11... | collective-permute-start | bytes 98312 | tf_op jit(solution)/shard_map/ppermute | solution.py:254
  4.9 0.8 %shard_map.101 = (bf16[256,384]{1,0:T(8,128)(2,1)S(1)}, bf16[256,384]{1,0:T(8,128)(2,1)S(1)}, f32[128,256]{1,0:T(8,128)S(1)}) custom-call(f32[4,256,256]{2,1,0:T(8,128)S(1)} %get-tuple-element.40.tq, f32[4,256,256]{2,1,0:T(8,128)S(1)} %get-tuple-element.41.te, f32[4,256,128]{2,1,0:T(8,128)S(1)} %get-tuple-element.42.tw), custom_call_target="tpu_custom_call" | custom-call | tf_op jit(solution)/shard_map/pallas_call | solution.py:54
  5.7 0.0 collective-permute-done.other
  5.7 0.2 shard_map.105
  5.9 2.7 %collective-permute-start.1 = (f32[64,128]{1,0:T(8,128)S(1)}, f32[64,128]{1,0:T(8,128)S(1)}, u32[]{:S(2)}, u32[]{:S(2)}) collective-permute-start(f32[64,128]{1,0:T(8,128)S(1)} %get-tuple-element.56.after.own), channel_id=1, source_target_pairs={{0,3},{1,2},{2,1},{3,0},{4,7},{5,6},{6,5},{7,4},{8,11},{9,10},{10,... | collective-permute-start | bytes 98312 | tf_op jit(solution)/shard_map/ppermute | solution.py:254
  8.6 0.9 %shard_map.102 = (bf16[256,384]{1,0:T(8,128)(2,1)S(1)}, bf16[256,384]{1,0:T(8,128)(2,1)S(1)}, f32[128,256]{1,0:T(8,128)S(1)}) custom-call(f32[4,256,256]{2,1,0:T(8,128)S(1)} %get-tuple-element.40.tq, f32[4,256,256]{2,1,0:T(8,128)S(1)} %get-tuple-element.41.te, f32[4,256,128]{2,1,0:T(8,128)S(1)} %get-tuple-element.42.tw, f32[128,256]{1,0:T(8,128)S(1)} %get-tuple-element.43.refs_0_), custom_call_target="tpu_custom_call" | custom-call | tf_op jit(solution)/shard_map/pallas_call | solution.py:54
  9.5 0.9 %shard_map.106.refs_1_.maps_a = f32[2,256,256]{2,1,0:T(8,128)S(1)} custom-call(f32[4,256,256]{2,1,0:T(8,128)S(1)} %get-tuple-element.58.q, f32[4,256,256]{2,1,0:T(8,128)S(1)} %get-tuple-element.59.e, f32[4,256,128]{2,1,0:T(8,128)S(1)} %get-tuple-element.60.w, f32[4,256,128]{2,1,0:T(8,128)S(1)} %get-tuple-element.61.y, f32[64,128]{1,0:T(8,128)S(1)} %get-tuple-element.56.after.own), custom_call_target="tpu_custom_call" | custom-call | tf_op jit(solution)/shard_map/pallas_call | solution.py:54
  10.5 0.0 collective-permute-done.1.other
  10.5 0.2 shard_map.107
  10.7 1.6 %collective-permute-start.2 = (f32[64,128]{1,0:T(8,128)S(1)}, f32[64,128]{1,0:T(8,128)S(1)}, u32[]{:S(2)}, u32[]{:S(2)}) collective-permute-start(f32[64,128]{1,0:T(8,128)S(1)} %get-tuple-element.62.after.own), channel_id=1, source_target_pairs={{0,5},{1,4},{2,7},{3,6},{4,1},{5,0},{6,3},{7,2},{8,13},{9,12},{10,... | collective-permute-start | bytes 98312 | tf_op jit(solution)/shard_map/ppermute | solution.py:254
  12.3 0.9 %shard_map.103 = (bf16[256,384]{1,0:T(8,128)(2,1)S(1)}, bf16[256,384]{1,0:T(8,128)(2,1)S(1)}, f32[128,256]{1,0:T(8,128)S(1)}) custom-call(f32[4,256,256]{2,1,0:T(8,128)S(1)} %get-tuple-element.40.tq, f32[4,256,256]{2,1,0:T(8,128)S(1)} %get-tuple-element.41.te, f32[4,256,128]{2,1,0:T(8,128)S(1)} %get-tuple-element.42.tw, f32[128,256]{1,0:T(8,128)S(1)} %get-tuple-element.44.refs_0_), custom_call_target="tpu_custom_call" | custom-call | tf_op jit(solution)/shard_map/pallas_call | solution.py:54
  13.2 0.9 %shard_map.108.refs_1_.maps_b = f32[2,256,256]{2,1,0:T(8,128)S(1)} custom-call(f32[4,256,256]{2,1,0:T(8,128)S(1)} %get-tuple-element.58.q, f32[4,256,256]{2,1,0:T(8,128)S(1)} %get-tuple-element.59.e, f32[4,256,128]{2,1,0:T(8,128)S(1)} %get-tuple-element.60.w, f32[4,256,128]{2,1,0:T(8,128)S(1)} %get-tuple-element.61.y, f32[64,128]{1,0:T(8,128)S(1)} %get-tuple-element.62.after.own), custom_call_target="tpu_custom_call" | custom-call | tf_op jit(solution)/shard_map/pallas_call | solution.py:54
  14.2 0.0 collective-permute-done.2.other
  14.2 0.2 shard_map.109
  14.4 2.6 %collective-permute-start.3 = (f32[64,128]{1,0:T(8,128)S(1)}, f32[64,128]{1,0:T(8,128)S(1)}, u32[]{:S(2)}, u32[]{:S(2)}) collective-permute-start(f32[64,128]{1,0:T(8,128)S(1)} %get-tuple-element.64.after.own), channel_id=1, source_target_pairs={{0,9},{1,8},{2,11},{3,10},{4,13},{5,12},{6,15},{7,14},{8,1},{9,0},... | collective-permute-start | bytes 98312 | tf_op jit(solution)/shard_map/ppermute | solution.py:254
  17.0 0.5 %shard_map.104 = (bf16[256,256]{1,0:T(8,128)(2,1)S(1)}, bf16[256,256]{1,0:T(8,128)(2,1)S(1)}) custom-call(f32[4,256,256]{2,1,0:T(8,128)S(1)} %get-tuple-element.40.tq, f32[4,256,256]{2,1,0:T(8,128)S(1)} %get-tuple-element.41.te, f32[4,256,128]{2,1,0:T(8,128)S(1)} %get-tuple-element.42.tw, f32[128,256]{1,0:T(8,128)S(1)} %get-tuple-element.45.refs_0_), custom_call_target="tpu_custom_call" | custom-call | tf_op jit(solution)/shard_map/pallas_call | solution.py:54
  17.5 1.3 %shard_map.110.refs_1_.node_maps = f32[3,256,256]{2,1,0:T(8,128)S(1)} custom-call(f32[3,256,256]{2,1,0:T(8,128)S(1)} %get-tuple-element.66.q, f32[3,256,256]{2,1,0:T(8,128)S(1)} %get-tuple-element.67.e, f32[3,256,128]{2,1,0:T(8,128)S(1)} %get-tuple-element.68.w, f32[3,256,128]{2,1,0:T(8,128)S(1)} %get-tuple-element.69.b, ...), custom_call_target="tpu_custom_call" | custom-call | tf_op jit(solution)/shard_map/pallas_call | solution.py:54
  18.9 0.0 collective-permute-done.3.other
  18.9 0.2 shard_map.111
  19.1 0.3 %collective-permute-start.4 = (f32[64,128]{1,0:T(8,128)S(1)}, f32[64,128]{1,0:T(8,128)S(1)}, u32[]{:S(2)}, u32[]{:S(2)}) collective-permute-start(f32[64,128]{1,0:T(8,128)S(1)} %get-tuple-element.72), channel_id=1, source_target_pairs={{0,1},{1,0},{2,3},{3,2},{4,5},{5,4},{6,7},{7,6},{8,9},{9,8},{10,11... | collective-permute-start | bytes 98312 | tf_op jit(solution)/shard_map/ppermute | solution.py:254
  19.4 0.7 %shard_map.112 = (f32[4,256,128]{2,1,0:T(8,128)S(1)}, bf16[4,256,256]{2,1,0:T(8,128)(2,1)S(1)}) custom-call(f32[3,256,256]{2,1,0:T(8,128)S(1)} %shard_map.110.refs_1_.node_maps, f32[2,256,256]{2,1,0:T(8,128)S(1)} %shard_map.106.refs_1_.maps_a, f32[2,256,256]{2,1,0:T(8,128)S(1)} %shard_map.108.refs_1_.maps_b, f32[64,128]{1,0:T(8,128)S(1)} %get-tuple-element.71.after.own), custom_call_target="tpu_custom_call" | custom-call | tf_op jit(solution)/shard_map/pallas_call | solution.py:54
  20.2 0.2 %collective-permute-done.4.other = f32[64,128]{1,0:T(8,128)S(1)} collective-permute-done((f32[64,128]{1,0:T(8,128)S(1)}, f32[64,128]{1,0:T(8,128)S(1)}, u32[]{:S(2)}, u32[]{:S(2)}) %collective-permute-start.4) | collective-permute-done | bytes 32800 | tf_op jit(solution)/shard_map/ppermute | solution.py:254
  20.4 1.1 %shard_map.113 = f32[4,256,128]{2,1,0:T(8,128)} custom-call(f32[64,128]{1,0:T(8,128)S(1)} %get-tuple-element.71.after.own, f32[64,128]{1,0:T(8,128)S(1)} %collective-permute-done.4.other, f32[4,256,128]{2,1,0:T(8,128)S(1)} %get-tuple-element.73.const, bf16[4,256,256]{2,1,0:T(8,128)(2,1)S(1)} %get-tuple-element.74.coef), custom_call_target="tpu_custom_call" | custom-call | tf_op jit(solution)/shard_map/pallas_call | solution.py:54
Async XLA Ops:
  4.3 1.4 %collective-permute-start = (f32[64,128]{1,0:T(8,128)S(1)}, f32[64,128]{1,0:T(8,128)S(1)}, u32[]{:S(2)}, u32[]{:S(2)}) collective-permute-start(f32[64,128]{1,0:T(8,128)S(1)} %get-tuple-element.55), channel_id=1, source_target_pairs={{0,1},{1,0},{2,3},{3,2},{4,5},{5,4},{6,7},{7,6},{8,9},{9,8},{10,11... | collective-permute-start | bytes 98312 | tf_op jit(solution)/shard_map/ppermute | solution.py:254
  5.9 4.6 %collective-permute-start.1 = (f32[64,128]{1,0:T(8,128)S(1)}, f32[64,128]{1,0:T(8,128)S(1)}, u32[]{:S(2)}, u32[]{:S(2)}) collective-permute-start(f32[64,128]{1,0:T(8,128)S(1)} %get-tuple-element.56.after.own), channel_id=1, source_target_pairs={{0,3},{1,2},{2,1},{3,0},{4,7},{5,6},{6,5},{7,4},{8,11},{9,10},{10,... | collective-permute-start | bytes 98312 | tf_op jit(solution)/shard_map/ppermute | solution.py:254
  10.7 3.5 %collective-permute-start.2 = (f32[64,128]{1,0:T(8,128)S(1)}, f32[64,128]{1,0:T(8,128)S(1)}, u32[]{:S(2)}, u32[]{:S(2)}) collective-permute-start(f32[64,128]{1,0:T(8,128)S(1)} %get-tuple-element.62.after.own), channel_id=1, source_target_pairs={{0,5},{1,4},{2,7},{3,6},{4,1},{5,0},{6,3},{7,2},{8,13},{9,12},{10,... | collective-permute-start | bytes 98312 | tf_op jit(solution)/shard_map/ppermute | solution.py:254
  14.4 4.5 %collective-permute-start.3 = (f32[64,128]{1,0:T(8,128)S(1)}, f32[64,128]{1,0:T(8,128)S(1)}, u32[]{:S(2)}, u32[]{:S(2)}) collective-permute-start(f32[64,128]{1,0:T(8,128)S(1)} %get-tuple-element.64.after.own), channel_id=1, source_target_pairs={{0,9},{1,8},{2,11},{3,10},{4,13},{5,12},{6,15},{7,14},{8,1},{9,0},... | collective-permute-start | bytes 98312 | tf_op jit(solution)/shard_map/ppermute | solution.py:254
  19.1 1.3 %collective-permute-start.4 = (f32[64,128]{1,0:T(8,128)S(1)}, f32[64,128]{1,0:T(8,128)S(1)}, u32[]{:S(2)}, u32[]{:S(2)}) collective-permute-start(f32[64,128]{1,0:T(8,128)S(1)} %get-tuple-element.72), channel_id=1, source_target_pairs={{0,1},{1,0},{2,3},{3,2},{4,5},{5,4},{6,7},{7,6},{8,9},{9,8},{10,11... | collective-permute-start | bytes 98312 | tf_op jit(solution)/shard_map/ppermute | solution.py:254

commit v3 on v2

--- a/solution.py
+++ b/solution.py
@@ -28,8 +28,14 @@
 
 def mul_narrow(a, b):
     m, n = a[0].shape[0], b[0].shape[1]
-    r = dot(jnp.concatenate(a, axis=0), jnp.concatenate(b, axis=1))
-    return r[:m, :n] + (r[:m, n:] + r[m:, :n])
+    step = 64
+    stack = [part[i : i + step] for i in range(0, m, step) for part in a]
+    r = dot(jnp.concatenate(stack, axis=0), jnp.concatenate(b, axis=1))
+    out = []
+    for i in range(0, 2 * m, 2 * step):
+        top, low = r[i : i + step], r[i + step : i + 2 * step]
+        out.append(top[:, :n] + (top[:, n:] + low[:, :n]))
+    return jnp.concatenate(out, axis=0)
 
 
 def mul_short(a, b):
@@ -72,7 +78,7 @@
 
 def up_kernel(
     levels, rhs, lq, le, lw, nq, ne, nw, tq, te, tw,
-    keep, send, yl, bn, eqn, lqv, lev, lwv, nqv, nev, nwv, tqv, tev, twv,
+    keep, send, yl, bn, lqv, lev, lwv, nqv, nev, nwv, tqv, tev, twv,
     rhsv, sems,
 ):
     leaves, nodes = rhs.shape[0], nq.shape[0]
@@ -85,36 +91,25 @@
         return copy
 
     got_b = start(rhs, rhsv)
-    got_q = [start(lq.at[i], lqv.at[i]) for i in range(leaves)]
-    got_nq, got_ne = start(nq, nqv), start(ne, nev)
-    got_e = [start(le.at[i], lev.at[i]) for i in range(leaves)]
-    got_lw, got_nw = start(lw, lwv), start(nw, nwv)
+    got_q = start(lq, lqv)
+    got_e = start(le, lev)
+    got_node = [start(nw, nwv), start(ne, nev), start(nq, nqv)]
+    got_lw = start(lw, lwv)
     got_top = [start(tq, tqv), start(te, tev), start(tw, twv)]
 
     got_b.wait()
-    mid, vals = [], []
-    for i in range(0, leaves, 2):
-        for j in (i, i + 1):
-            got_q[j].wait()
-        for j in (i, i + 1):
-            mid.append(split(mul_narrow(split(lqv[j]), split(rhsv[j]))))
-    got_nq.wait()
-    got_ne.wait()
-    eqs = []
-    for i in range(nodes):
-        eq = mul(split(nev[i]), split(nqv[i]))
-        eqn[i] = eq
-        eqs.append(split(eq))
-    for i in range(0, leaves, 2):
-        for j in (i, i + 1):
-            got_e[j].wait()
-        for j in (i, i + 1):
-            y = mul_narrow(split(lev[j]), mid[j])
-            yl[j] = y
-            vals.append(split(y))
-    got_lw.wait()
-    got_nw.wait()
-    maps = [split(mul(split(nwv[i].T), eqs[i])) for i in range(nodes)]
+    got_q.wait()
+    mid = [split(mul_narrow(split(lqv[i]), split(rhsv[i]))) for i in range(leaves)]
+    got_e.wait()
+    vals = []
+    for i in range(leaves):
+        y = mul_narrow(split(lev[i]), mid[i])
+        yl[i] = y
+        vals.append(split(y))
+    for copy in got_node + [got_lw]:
+        copy.wait()
+    half_maps = [split(mul(split(nwv[i].T), split(nev[i]))) for i in range(nodes)]
+    maps = [split(mul(half_maps[i], split(nqv[i]))) for i in range(nodes)]
     reduced = [mul_narrow(split(lwv[i].T), vals[i]) for i in range(leaves)]
     offset = 0
     while len(reduced) > 1:
@@ -141,6 +136,7 @@
     at = level - 1
     if last:
         c = mul(split(te[at, half, :]), split(tq[at])).T
+        yield
         if not first:
             c = mul(split(c), split(refs[0][...]))
         outs[0][...], outs[1][...] = split(c)
@@ -148,6 +144,7 @@
     e, w = split(te[at]), split(tw[at])
     x = mul(e, split(tq[at]))
     z = mul_narrow(e, w)
+    yield
     if first:
         q = split(tq[at])
         outs[0][...], outs[1][...] = split(mul(split(x.T), beside(w, q)))
@@ -156,6 +153,7 @@
     q = split(tq[at, :, half])
     both = mul(split(x.T), beside(w, q))
     g = mul_narrow(split(z.T), q)
+    yield
     low = mul(split(jnp.concatenate([both[:, width:], g], axis=0)), split(refs[0][...]))
     a = split(both[:, :width])
     tb = split(low[: 2 * width])
@@ -193,25 +191,29 @@
 
 
 def leaf_kernel(begin, q, e, w, y, after, out):
-    for i in range(out.shape[0]):
-        at = begin + i
-        ew = mul_narrow(split(e[at]), split(w[at]))
-        out[i] = mul(split(q[at].T), beside(split(y[at]), split(ew)))
-
-
-def node_kernel(q, e, w, b, eq, after, out):
-    for i in range(out.shape[0]):
-        y = mul_narrow(split(eq[i]), split(b[i]))
-        ew = mul_narrow(split(e[i]), split(w[i]))
-        out[i] = mul(split(q[i].T), beside(split(y), split(ew)))
-
-
-def compose_kernel(node_maps, maps_a, maps_b, after, const, coef):
-    nodes = node_maps.shape[0]
+    run = range(out.shape[0])
+    ew = [split(mul_narrow(split(e[begin + i]), split(w[begin + i]))) for i in run]
+    yield
+    for i in run:
+        out[i] = mul(split(q[begin + i].T), beside(split(y[begin + i]), ew[i]))
+
+
+def node_kernel(begin, q, e, w, b, after, out):
+    run = range(out.shape[0])
+    t = [split(mul_narrow(split(q[begin + i]), split(b[begin + i]))) for i in run]
+    yield
+    y_ew = [split(mul(split(e[begin + i]), beside(t[i], split(w[begin + i])))) for i in run]
+    yield
+    for i in run:
+        out[i] = mul(split(q[begin + i].T), y_ew[i])
+
+
+def compose_kernel(maps_a, root_map, maps_b, node_maps, after, const, coef):
+    nodes = node_maps.shape[0] + 1
     half = maps_a.shape[0]
     cols = const.shape[2]
     width = maps_a.shape[2] - cols
-    top = node_maps[nodes - 1]
+    top = root_map[0]
     parent = [jnp.concatenate([top[:, :cols], -top[:, cols:]], axis=1)]
 
     def below(vg, j):
@@ -247,6 +249,34 @@
     for i in range(out.shape[0]):
         moved = dot(coef[i], g, 1)
         out[i] = const[i] + (moved[:, :cols] + moved[:, cols:])
+
+
+def window_kernel(parts, *refs):
+    taken = sum(n_in for _, n_in, _ in parts)
+    given = taken
+    at = 0
+    running = []
+    for part, n_in, n_out in parts:
+        running.append(part(*refs[at : at + n_in], *refs[given : given + n_out]))
+        at += n_in
+        given += n_out
+    while running:
+        running = [job for job in running if next(job, True) is None]
+
+
+def together(*jobs):
+    parts = [(kernel, len(ins), len(outs)) for kernel, outs, ins in jobs]
+    outs = [o for _, o, _ in jobs]
+    flat = call(
+        functools.partial(window_kernel, parts),
+        sum(outs, []),
+        sum([ins for _, _, ins in jobs], []),
+    )
+    results = []
+    for o in outs:
+        results.append(flat[: len(o)])
+        flat = flat[len(o) :]
+    return results
 
 
 def swapped(value, mask):
@@ -267,55 +297,57 @@
             ((cols // 2, width), F32),
             (rhs.shape, F32),
             ((nodes, size, cols), F32),
-            (node_q.shape, F32),
         ]
         + [(a.shape, F32) for a in weights],
         [rhs] + weights,
-        scratch=[pltpu.VMEM(rhs.shape, F32), pltpu.SemaphoreType.DMA((2 * leaves + 8,))],
+        scratch=[pltpu.VMEM(rhs.shape, F32), pltpu.SemaphoreType.DMA((10,))],
         hbm_ins=range(10),
     )
-    block, sent, yl, bn, eqn, lq, le, lw, nq, ne, nw, tq, te, tw = res
+    block, sent, yl, bn, lq, le, lw, nq, ne, nw, tq, te, tw = res
 
     half = leaves // 2
-    leaf_map = lambda begin, after: call(
-        functools.partial(leaf_kernel, begin),
-        [((half, size, cols + width), F32)],
-        [lq, le, lw, yl, after],
-    )
-    trans, k, maps, done = [], [], [], []
+    plan = {
+        2: [(leaf_kernel, 0, half), (node_kernel, nodes - 1, 1)],
+        3: [(leaf_kernel, half, half)],
+        levels: [(node_kernel, 0, nodes - 1)],
+    }
+    trans, k, maps = [], [], []
     for level in range(1, levels + 1):
         last = level == levels
         other = swapped(sent if level == 1 else block, 2 ** (level - 1) | 1)
         wide = 2 * width if last else 3 * width
-        outs = [((size, wide), BF16)] * 2 + ([] if last else [((width, size), F32)])
-        made = call(
-            functools.partial(level_kernel, level, levels), outs, [tq, te, tw] + trans
-        )
-        trans = list(made[2:])
-        done = []
-        if level == min(2, levels):
-            done += leaf_map(0, block)
-        if level == min(3, levels):
-            done += leaf_map(half, block)
-        maps += done
-        if last:
-            node_maps = call(
-                node_kernel,
-                [((nodes, size, cols + width), F32)],
-                [nq, ne, nw, bn, eqn, block],
+        jobs = [
+            (
+                functools.partial(level_kernel, level, levels),
+                [((size, wide), BF16)] * 2 + ([] if last else [((width, size), F32)]),
+                [tq, te, tw] + trans,
             )
-            done += node_maps
+        ]
+        if level in plan:
+            for kernel, begin, count in plan[level]:
+                ins = [lq, le, lw, yl] if kernel is leaf_kernel else [nq, ne, nw, bn]
+                jobs.append(
+                    (
+                        functools.partial(kernel, begin),
+                        [((count, size, cols + width), F32)],
+                        ins + [block],
+                    )
+                )
+        made, *chores = together(*jobs)
+        trans = made[2:]
+        chores = [c[0] for c in chores]
+        maps += chores
         block, k_new = call(
             functools.partial(root_kernel if last else step_kernel, level),
             [((cols // 2, width), F32), ((cols // 2, width if last else size), F32)],
-            [made[0], made[1], block, other] + k + done,
+            [made[0], made[1], block, other] + k + chores,
         )
         k = [k_new]
     other = swapped(k[0], 1)
     const, coef = call(
         compose_kernel,
         [((leaves, size, cols), F32), ((leaves, size, 2 * width), BF16)],
-        node_maps + maps + [block],
+        maps + [block],
     )
     return call(
         functools.partial(final_kernel, levels),

time: 21.7 us -> 20.7 us (0.954)
  Pallas kernels: 13.4 us -> 10.7 us
  waiting for transfers between devices: 0.23 us -> 1.42 us
  starting transfers between devices: 7.75 us -> 8.33 us
    pallas_call x14 -> x11, Pallas kernels: 13.4 us -> 10.7 us  [call(): pl.pallas_call(kernel, out_shape=[jax.ShapeDtypeStruct(s, d) for s, d in...]
    ppermute x5, waiting for transfers between devices: 0.23 us -> 1.42 us  [swapped(): return lax.ppermute(value, 'leaf', pairs)]
    ppermute x5, starting transfers between devices: 7.75 us -> 8.33 us  [swapped(): return lax.ppermute(value, 'leaf', pairs)]
  transfers between devices with their start and end apart: 5 -> 5, of which waited for: 1 -> 4; matrix products, arithmetic and copies ran while one was open for 0% -> 0% of each run, Pallas kernels for 33% -> 25%
where the time goes in v3:
time: 20.7 us; the launch traced here: 20.5 us
  Pallas kernels  10.7 us (52%)
  starting transfers between devices  8.33 us (40%)
  waiting for transfers between devices  1.42 us (7%)
    pallas_call x11, Pallas kernels, call(): pl.pallas_call(kernel, out_shape=[jax.ShapeDtypeStruct(s, d) for s, d in...  10.7 us
    ppermute x5, starting transfers between devices, swapped(): return lax.ppermute(value, 'leaf', pairs)  8.33 us
    ppermute x5, waiting for transfers between devices, swapped(): return lax.ppermute(value, 'leaf', pairs)  1.42 us
  transfers between devices with their start and end apart: 5, of which 4 were waited for; matrix products, arithmetic and copies ran while one was open for 0% of the time, Pallas kernels for 25%

profile of v3, /device:TPU:0, one launch (start us, length us, event | category | flops | bytes accessed | tf_op | source)
XLA Modules:
  0.0 20.5 jit_solution(7649744656609945325)
XLA Ops:
  0.0 3.7 %shard_map.100 = (f32[64,128]{1,0:T(8,128)S(1)}, f32[64,128]{1,0:T(8,128)S(1)}, f32[4,256,128]{2,1,0:T(8,128)S(1)}, f32[3,256,128]{2,1,0:T(8,128)S(1)}, f32[4,25...) custom-call(f32[4,256,128]{2,1,0:T(8,128)} %rhs.1, ...), custom_call_target="tpu_custom_call" | custom-call | tf_op jit(solution)/shard_map/pallas_call | solution.py:60
  3.7 0.6 %collective-permute-start = (f32[64,128]{1,0:T(8,128)S(1)}, f32[64,128]{1,0:T(8,128)S(1)}, u32[]{:S(2)}, u32[]{:S(2)}) collective-permute-start(f32[64,128]{1,0:T(8,128)S(1)} %get-tuple-element.54), channel_id=1, source_target_pairs={{0,1},{1,0},{2,3},{3,2},{4,5},{5,4},{6,7},{7,6},{8,9},{9,8},{10,11... | collective-permute-start | bytes 98312 | tf_op jit(solution)/shard_map/ppermute | solution.py:284
  4.3 0.8 %shard_map.101 = (bf16[256,384]{1,0:T(8,128)(2,1)S(1)}, bf16[256,384]{1,0:T(8,128)(2,1)S(1)}, f32[128,256]{1,0:T(8,128)S(1)}) custom-call(f32[4,256,256]{2,1,0:T(8,128)S(1)} %get-tuple-element.43.refs_0_, f32[4,256,256]{2,1,0:T(8,128)S(1)} %get-tuple-element.44.refs_1_, f32[4,256,128]{2,1,0:T(8,128)S(1)} %get-tuple-element.45.refs_2_), custom_call_target="tpu_custom_call" | custom-call | tf_op jit(solution)/shard_map/pallas_call | solution.py:60
  5.1 0.0 collective-permute-done.other
  5.1 0.2 shard_map.102
  5.3 2.7 %collective-permute-start.1 = (f32[64,128]{1,0:T(8,128)S(1)}, f32[64,128]{1,0:T(8,128)S(1)}, u32[]{:S(2)}, u32[]{:S(2)}) collective-permute-start(f32[64,128]{1,0:T(8,128)S(1)} %get-tuple-element.55.refs_8_.refs_13_.own), channel_id=1, source_target_pairs={{0,3},{1,2},{2,1},{3,0},{4,7},{5,6},{6,5},{7,4},{8,11},{9,10},{10,... | collective-permute-start | bytes 98312 | tf_op jit(solution)/shard_map/ppermute | solution.py:284
  8.0 1.4 %shard_map.103 = (bf16[256,384]{1,0:T(8,128)(2,1)S(1)}, bf16[256,384]{1,0:T(8,128)(2,1)S(1)}, f32[128,256]{1,0:T(8,128)S(1)}, f32[2,256,256]{2,1,0:T(8,128)S(1)}, f32[1,256,256]{2,1,0:T(8,128)S(1)}) custom-call(f32[4,256,256]{2,1,0:T(8,128)S(1)} %get-tuple-element.43.refs_0_, f32[4,256,256]{2,1,0:T(8,128)S(1)} %get-tuple-element.44.refs_1_, ...), custom_call_target="tpu_custom_call" | custom-call | tf_op jit(solution)/shard_map/pallas_call | solution.py:60
  9.4 0.2 %collective-permute-done.1.other = f32[64,128]{1,0:T(8,128)S(1)} collective-permute-done((f32[64,128]{1,0:T(8,128)S(1)}, f32[64,128]{1,0:T(8,128)S(1)}, u32[]{:S(2)}, u32[]{:S(2)}) %collective-permute-start.1) | collective-permute-done | bytes 32800 | tf_op jit(solution)/shard_map/ppermute | solution.py:284
  9.6 0.2 shard_map.104
  9.8 1.9 %collective-permute-start.2 = (f32[64,128]{1,0:T(8,128)S(1)}, f32[64,128]{1,0:T(8,128)S(1)}, u32[]{:S(2)}, u32[]{:S(2)}) collective-permute-start(f32[64,128]{1,0:T(8,128)S(1)} %get-tuple-element.66.refs_8_.own), channel_id=1, source_target_pairs={{0,5},{1,4},{2,7},{3,6},{4,1},{5,0},{6,3},{7,2},{8,13},{9,12},{10,... | collective-permute-start | bytes 98312 | tf_op jit(solution)/shard_map/ppermute | solution.py:284
  11.7 1.1 %shard_map.105 = (bf16[256,384]{1,0:T(8,128)(2,1)S(1)}, bf16[256,384]{1,0:T(8,128)(2,1)S(1)}, f32[128,256]{1,0:T(8,128)S(1)}, f32[2,256,256]{2,1,0:T(8,128)S(1)}) custom-call(f32[4,256,256]{2,1,0:T(8,128)S(1)} %get-tuple-element.43.refs_0_, f32[4,256,256]{2,1,0:T(8,128)S(1)} %get-tuple-element.44.refs_1_, f32[4,256,128]{2,1,0:T(8,128)S(1)} %get-tuple-element.45.refs_2_, ...), custom_call_target="tpu_custom_call" | custom-call | tf_op jit(solution)/shard_map/pallas_call | solution.py:60
  12.8 0.5 %collective-permute-done.2.other = f32[64,128]{1,0:T(8,128)S(1)} collective-permute-done((f32[64,128]{1,0:T(8,128)S(1)}, f32[64,128]{1,0:T(8,128)S(1)}, u32[]{:S(2)}, u32[]{:S(2)}) %collective-permute-start.2) | collective-permute-done | bytes 32800 | tf_op jit(solution)/shard_map/ppermute | solution.py:284
  13.3 0.2 shard_map.106
  13.5 2.8 %collective-permute-start.3 = (f32[64,128]{1,0:T(8,128)S(1)}, f32[64,128]{1,0:T(8,128)S(1)}, u32[]{:S(2)}, u32[]{:S(2)}) collective-permute-start(f32[64,128]{1,0:T(8,128)S(1)} %get-tuple-element.72.refs_8_.own), channel_id=1, source_target_pairs={{0,9},{1,8},{2,11},{3,10},{4,13},{5,12},{6,15},{7,14},{8,1},{9,0},... | collective-permute-start | bytes 98312 | tf_op jit(solution)/shard_map/ppermute | solution.py:284
  16.3 1.1 %shard_map.107 = (bf16[256,256]{1,0:T(8,128)(2,1)S(1)}, bf16[256,256]{1,0:T(8,128)(2,1)S(1)}, f32[2,256,256]{2,1,0:T(8,128)S(1)}) custom-call(f32[4,256,256]{2,1,0:T(8,128)S(1)} %get-tuple-element.43.refs_0_, f32[4,256,256]{2,1,0:T(8,128)S(1)} %get-tuple-element.44.refs_1_, f32[4,256,128]{2,1,0:T(8,128)S(1)} %get-tuple-element.45.refs_2_, ...), custom_call_target="tpu_custom_call" | custom-call | tf_op jit(solution)/shard_map/pallas_call | solution.py:60
  17.4 0.5 %collective-permute-done.3.other = f32[64,128]{1,0:T(8,128)S(1)} collective-permute-done((f32[64,128]{1,0:T(8,128)S(1)}, f32[64,128]{1,0:T(8,128)S(1)}, u32[]{:S(2)}, u32[]{:S(2)}) %collective-permute-start.3) | collective-permute-done | bytes 32800 | tf_op jit(solution)/shard_map/ppermute | solution.py:284
  17.9 0.2 shard_map.108
  18.1 0.4 %collective-permute-start.4 = (f32[64,128]{1,0:T(8,128)S(1)}, f32[64,128]{1,0:T(8,128)S(1)}, u32[]{:S(2)}, u32[]{:S(2)}) collective-permute-start(f32[64,128]{1,0:T(8,128)S(1)} %get-tuple-element.78), channel_id=1, source_target_pairs={{0,1},{1,0},{2,3},{3,2},{4,5},{5,4},{6,7},{7,6},{8,9},{9,8},{10,11... | collective-permute-start | bytes 98312 | tf_op jit(solution)/shard_map/ppermute | solution.py:284
  18.5 0.7 %shard_map.109 = (f32[4,256,128]{2,1,0:T(8,128)S(1)}, bf16[4,256,256]{2,1,0:T(8,128)(2,1)S(1)}) custom-call(f32[2,256,256]{2,1,0:T(8,128)S(1)} %get-tuple-element.64.refs_1_.maps_a, f32[1,256,256]{2,1,0:T(8,128)S(1)} %get-tuple-element.65.refs_2_.root_map, f32[2,256,256]{2,1,0:T(8,128)S(1)} %get-tuple-element.71.refs_1_.maps_b, ...), custom_call_target="tpu_custom_call" | custom-call | tf_op jit(solution)/shard_map/pallas_call | solution.py:60
  19.3 0.2 collective-permute-done.4.other
  19.4 1.1 %shard_map.110 = f32[4,256,128]{2,1,0:T(8,128)} custom-call(f32[64,128]{1,0:T(8,128)S(1)} %get-tuple-element.77.after.own, f32[64,128]{1,0:T(8,128)S(1)} %collective-permute-done.4.other, f32[4,256,128]{2,1,0:T(8,128)S(1)} %get-tuple-element.79.const, bf16[4,256,256]{2,1,0:T(8,128)(2,1)S(1)} %get-tuple-element.80.coef), custom_call_target="tpu_custom_call" | custom-call | tf_op jit(solution)/shard_map/pallas_call | solution.py:60
Async XLA Ops:
  3.7 1.4 %collective-permute-start = (f32[64,128]{1,0:T(8,128)S(1)}, f32[64,128]{1,0:T(8,128)S(1)}, u32[]{:S(2)}, u32[]{:S(2)}) collective-permute-start(f32[64,128]{1,0:T(8,128)S(1)} %get-tuple-element.54), channel_id=1, source_target_pairs={{0,1},{1,0},{2,3},{3,2},{4,5},{5,4},{6,7},{7,6},{8,9},{9,8},{10,11... | collective-permute-start | bytes 98312 | tf_op jit(solution)/shard_map/ppermute | solution.py:284
  5.3 4.3 %collective-permute-start.1 = (f32[64,128]{1,0:T(8,128)S(1)}, f32[64,128]{1,0:T(8,128)S(1)}, u32[]{:S(2)}, u32[]{:S(2)}) collective-permute-start(f32[64,128]{1,0:T(8,128)S(1)} %get-tuple-element.55.refs_8_.refs_13_.own), channel_id=1, source_target_pairs={{0,3},{1,2},{2,1},{3,0},{4,7},{5,6},{6,5},{7,4},{8,11},{9,10},{10,... | collective-permute-start | bytes 98312 | tf_op jit(solution)/shard_map/ppermute | solution.py:284
  9.8 3.5 %collective-permute-start.2 = (f32[64,128]{1,0:T(8,128)S(1)}, f32[64,128]{1,0:T(8,128)S(1)}, u32[]{:S(2)}, u32[]{:S(2)}) collective-permute-start(f32[64,128]{1,0:T(8,128)S(1)} %get-tuple-element.66.refs_8_.own), channel_id=1, source_target_pairs={{0,5},{1,4},{2,7},{3,6},{4,1},{5,0},{6,3},{7,2},{8,13},{9,12},{10,... | collective-permute-start | bytes 98312 | tf_op jit(solution)/shard_map/ppermute | solution.py:284
  13.5 4.4 %collective-permute-start.3 = (f32[64,128]{1,0:T(8,128)S(1)}, f32[64,128]{1,0:T(8,128)S(1)}, u32[]{:S(2)}, u32[]{:S(2)}) collective-permute-start(f32[64,128]{1,0:T(8,128)S(1)} %get-tuple-element.72.refs_8_.own), channel_id=1, source_target_pairs={{0,9},{1,8},{2,11},{3,10},{4,13},{5,12},{6,15},{7,14},{8,1},{9,0},... | collective-permute-start | bytes 98312 | tf_op jit(solution)/shard_map/ppermute | solution.py:284
  18.1 1.3 %collective-permute-start.4 = (f32[64,128]{1,0:T(8,128)S(1)}, f32[64,128]{1,0:T(8,128)S(1)}, u32[]{:S(2)}, u32[]{:S(2)}) collective-permute-start(f32[64,128]{1,0:T(8,128)S(1)} %get-tuple-element.78), channel_id=1, source_target_pairs={{0,1},{1,0},{2,3},{3,2},{4,5},{5,4},{6,7},{7,6},{8,9},{9,8},{10,11... | collective-permute-start | bytes 98312 | tf_op jit(solution)/shard_map/ppermute | solution.py:284

commit v4 on v3

--- a/solution.py
+++ b/solution.py
@@ -48,7 +48,7 @@
     return tuple(jnp.concatenate(parts, axis=1) for parts in zip(*pairs))
 
 
-def call(kernel, outs, ins, scratch=(), hbm_ins=()):
+def call(kernel, outs, ins, scratch=(), hbm_ins=(), out_space=pltpu.VMEM):
     specs = [
         pl.BlockSpec(memory_space=pltpu.HBM if i in hbm_ins else pltpu.VMEM)
         for i in range(len(ins))
@@ -61,7 +61,7 @@
         kernel,
         out_shape=[jax.ShapeDtypeStruct(s, d) for s, d in outs],
         in_specs=specs,
-        out_specs=[pl.BlockSpec(memory_space=pltpu.VMEM) for _ in outs],
+        out_specs=[pl.BlockSpec(memory_space=out_space) for _ in outs],
         scratch_shapes=list(scratch),
         compiler_params=pltpu.CompilerParams(vmem_limit_bytes=24 << 20),
     )(*ins)
@@ -109,8 +109,8 @@
     for copy in got_node + [got_lw]:
         copy.wait()
     half_maps = [split(mul(split(nwv[i].T), split(nev[i]))) for i in range(nodes)]
+    reduced = [mul_narrow(split(lwv[i].T), vals[i]) for i in range(leaves)]
     maps = [split(mul(half_maps[i], split(nqv[i]))) for i in range(nodes)]
-    reduced = [mul_narrow(split(lwv[i].T), vals[i]) for i in range(leaves)]
     offset = 0
     while len(reduced) > 1:
         count = len(reduced) // 2
@@ -232,7 +232,7 @@
         coef[i] = jnp.concatenate(split(full[:, cols:]), axis=1)
 
 
-def final_kernel(levels, own, other, const, coef, out):
+def final_kernel(levels, own, other, const, coef, out, held, sems):
     low = columns_of(levels) == 0
     a, b = own[...], other[...]
     hi, lo = split(
@@ -246,9 +246,14 @@
         ],
         axis=0,
     )
+    copies = []
     for i in range(out.shape[0]):
         moved = dot(coef[i], g, 1)
-        out[i] = const[i] + (moved[:, :cols] + moved[:, cols:])
+        held[i] = const[i] + (moved[:, :cols] + moved[:, cols:])
+        copies.append(pltpu.make_async_copy(held.at[i], out.at[i], sems.at[i]))
+        copies[i].start()
+    for copy in copies:
+        copy.wait()
 
 
 def window_kernel(parts, *refs):
@@ -353,6 +358,8 @@
         functools.partial(final_kernel, levels),
         [((leaves, size, cols), F32)],
         [block, other, const, coef],
+        scratch=[pltpu.VMEM(rhs.shape, F32), pltpu.SemaphoreType.DMA((leaves,))],
+        out_space=pltpu.HBM,
     )[0]
 
 

time: 20.7 us -> 20.6 us (level)
  no operation moved by 1% of the time
where the time goes in v4:
time: 20.6 us; the launch traced here: 20.4 us
  Pallas kernels  10.5 us (51%)
  starting transfers between devices  8.33 us (40%)
  waiting for transfers between devices  1.43 us (7%)
    pallas_call x11, Pallas kernels, call(): pl.pallas_call(kernel, out_shape=[jax.ShapeDtypeStruct(s, d) for s, d in...  10.5 us
    ppermute x5, starting transfers between devices, swapped(): return lax.ppermute(value, 'leaf', pairs)  8.33 us
    ppermute x5, waiting for transfers between devices, swapped(): return lax.ppermute(value, 'leaf', pairs)  1.43 us
  transfers between devices with their start and end apart: 5, of which 4 were waited for; matrix products, arithmetic and copies ran while one was open for 0% of the time, Pallas kernels for 25%

profile of v4, /device:TPU:0, one launch (start us, length us, event | category | flops | bytes accessed | tf_op | source)
XLA Modules:
  0.0 20.4 jit_solution(9456189814006045120)
XLA Ops:
  0.0 3.6 %shard_map.100 = (f32[64,128]{1,0:T(8,128)S(1)}, f32[64,128]{1,0:T(8,128)S(1)}, f32[4,256,128]{2,1,0:T(8,128)S(1)}, f32[3,256,128]{2,1,0:T(8,128)S(1)}, f32[4,25...) custom-call(f32[4,256,128]{2,1,0:T(8,128)} %rhs.1, ...), custom_call_target="tpu_custom_call" | custom-call | tf_op jit(solution)/shard_map/pallas_call | solution.py:60
  3.6 0.6 %collective-permute-start = (f32[64,128]{1,0:T(8,128)S(1)}, f32[64,128]{1,0:T(8,128)S(1)}, u32[]{:S(2)}, u32[]{:S(2)}) collective-permute-start(f32[64,128]{1,0:T(8,128)S(1)} %get-tuple-element.54), channel_id=1, source_target_pairs={{0,1},{1,0},{2,3},{3,2},{4,5},{5,4},{6,7},{7,6},{8,9},{9,8},{10,11... | collective-permute-start | bytes 98312 | tf_op jit(solution)/shard_map/ppermute | solution.py:289
  4.1 0.8 %shard_map.101 = (bf16[256,384]{1,0:T(8,128)(2,1)S(1)}, bf16[256,384]{1,0:T(8,128)(2,1)S(1)}, f32[128,256]{1,0:T(8,128)S(1)}) custom-call(f32[4,256,256]{2,1,0:T(8,128)S(1)} %get-tuple-element.43.refs_0_, f32[4,256,256]{2,1,0:T(8,128)S(1)} %get-tuple-element.44.refs_1_, f32[4,256,128]{2,1,0:T(8,128)S(1)} %get-tuple-element.45.refs_2_), custom_call_target="tpu_custom_call" | custom-call | tf_op jit(solution)/shard_map/pallas_call | solution.py:60
  5.0 0.0 collective-permute-done.other
  5.0 0.2 shard_map.102
  5.2 2.7 %collective-permute-start.1 = (f32[64,128]{1,0:T(8,128)S(1)}, f32[64,128]{1,0:T(8,128)S(1)}, u32[]{:S(2)}, u32[]{:S(2)}) collective-permute-start(f32[64,128]{1,0:T(8,128)S(1)} %get-tuple-element.55.refs_8_.refs_13_.own), channel_id=1, source_target_pairs={{0,3},{1,2},{2,1},{3,0},{4,7},{5,6},{6,5},{7,4},{8,11},{9,10},{10,... | collective-permute-start | bytes 98312 | tf_op jit(solution)/shard_map/ppermute | solution.py:289
  7.9 1.4 %shard_map.103 = (bf16[256,384]{1,0:T(8,128)(2,1)S(1)}, bf16[256,384]{1,0:T(8,128)(2,1)S(1)}, f32[128,256]{1,0:T(8,128)S(1)}, f32[2,256,256]{2,1,0:T(8,128)S(1)}, f32[1,256,256]{2,1,0:T(8,128)S(1)}) custom-call(f32[4,256,256]{2,1,0:T(8,128)S(1)} %get-tuple-element.43.refs_0_, f32[4,256,256]{2,1,0:T(8,128)S(1)} %get-tuple-element.44.refs_1_, ...), custom_call_target="tpu_custom_call" | custom-call | tf_op jit(solution)/shard_map/pallas_call | solution.py:60
  9.3 0.2 %collective-permute-done.1.other = f32[64,128]{1,0:T(8,128)S(1)} collective-permute-done((f32[64,128]{1,0:T(8,128)S(1)}, f32[64,128]{1,0:T(8,128)S(1)}, u32[]{:S(2)}, u32[]{:S(2)}) %collective-permute-start.1) | collective-permute-done | bytes 32800 | tf_op jit(solution)/shard_map/ppermute | solution.py:289
  9.5 0.2 shard_map.104
  9.7 1.9 %collective-permute-start.2 = (f32[64,128]{1,0:T(8,128)S(1)}, f32[64,128]{1,0:T(8,128)S(1)}, u32[]{:S(2)}, u32[]{:S(2)}) collective-permute-start(f32[64,128]{1,0:T(8,128)S(1)} %get-tuple-element.66.refs_8_.own), channel_id=1, source_target_pairs={{0,5},{1,4},{2,7},{3,6},{4,1},{5,0},{6,3},{7,2},{8,13},{9,12},{10,... | collective-permute-start | bytes 98312 | tf_op jit(solution)/shard_map/ppermute | solution.py:289
  11.6 1.1 %shard_map.105 = (bf16[256,384]{1,0:T(8,128)(2,1)S(1)}, bf16[256,384]{1,0:T(8,128)(2,1)S(1)}, f32[128,256]{1,0:T(8,128)S(1)}, f32[2,256,256]{2,1,0:T(8,128)S(1)}) custom-call(f32[4,256,256]{2,1,0:T(8,128)S(1)} %get-tuple-element.43.refs_0_, f32[4,256,256]{2,1,0:T(8,128)S(1)} %get-tuple-element.44.refs_1_, f32[4,256,128]{2,1,0:T(8,128)S(1)} %get-tuple-element.45.refs_2_, ...), custom_call_target="tpu_custom_call" | custom-call | tf_op jit(solution)/shard_map/pallas_call | solution.py:60
  12.6 0.5 %collective-permute-done.2.other = f32[64,128]{1,0:T(8,128)S(1)} collective-permute-done((f32[64,128]{1,0:T(8,128)S(1)}, f32[64,128]{1,0:T(8,128)S(1)}, u32[]{:S(2)}, u32[]{:S(2)}) %collective-permute-start.2) | collective-permute-done | bytes 32800 | tf_op jit(solution)/shard_map/ppermute | solution.py:289
  13.2 0.2 shard_map.106
  13.4 2.8 %collective-permute-start.3 = (f32[64,128]{1,0:T(8,128)S(1)}, f32[64,128]{1,0:T(8,128)S(1)}, u32[]{:S(2)}, u32[]{:S(2)}) collective-permute-start(f32[64,128]{1,0:T(8,128)S(1)} %get-tuple-element.72.refs_8_.own), channel_id=1, source_target_pairs={{0,9},{1,8},{2,11},{3,10},{4,13},{5,12},{6,15},{7,14},{8,1},{9,0},... | collective-permute-start | bytes 98312 | tf_op jit(solution)/shard_map/ppermute | solution.py:289
  16.2 1.1 %shard_map.107 = (bf16[256,256]{1,0:T(8,128)(2,1)S(1)}, bf16[256,256]{1,0:T(8,128)(2,1)S(1)}, f32[2,256,256]{2,1,0:T(8,128)S(1)}) custom-call(f32[4,256,256]{2,1,0:T(8,128)S(1)} %get-tuple-element.43.refs_0_, f32[4,256,256]{2,1,0:T(8,128)S(1)} %get-tuple-element.44.refs_1_, f32[4,256,128]{2,1,0:T(8,128)S(1)} %get-tuple-element.45.refs_2_, ...), custom_call_target="tpu_custom_call" | custom-call | tf_op jit(solution)/shard_map/pallas_call | solution.py:60
  17.3 0.5 %collective-permute-done.3.other = f32[64,128]{1,0:T(8,128)S(1)} collective-permute-done((f32[64,128]{1,0:T(8,128)S(1)}, f32[64,128]{1,0:T(8,128)S(1)}, u32[]{:S(2)}, u32[]{:S(2)}) %collective-permute-start.3) | collective-permute-done | bytes 32800 | tf_op jit(solution)/shard_map/ppermute | solution.py:289
  17.8 0.2 shard_map.108
  18.0 0.4 %collective-permute-start.4 = (f32[64,128]{1,0:T(8,128)S(1)}, f32[64,128]{1,0:T(8,128)S(1)}, u32[]{:S(2)}, u32[]{:S(2)}) collective-permute-start(f32[64,128]{1,0:T(8,128)S(1)} %get-tuple-element.78), channel_id=1, source_target_pairs={{0,1},{1,0},{2,3},{3,2},{4,5},{5,4},{6,7},{7,6},{8,9},{9,8},{10,11... | collective-permute-start | bytes 98312 | tf_op jit(solution)/shard_map/ppermute | solution.py:289
  18.4 0.7 %shard_map.109 = (f32[4,256,128]{2,1,0:T(8,128)S(1)}, bf16[4,256,256]{2,1,0:T(8,128)(2,1)S(1)}) custom-call(f32[2,256,256]{2,1,0:T(8,128)S(1)} %get-tuple-element.64.refs_1_.maps_a, f32[1,256,256]{2,1,0:T(8,128)S(1)} %get-tuple-element.65.refs_2_.root_map, f32[2,256,256]{2,1,0:T(8,128)S(1)} %get-tuple-element.71.refs_1_.maps_b, ...), custom_call_target="tpu_custom_call" | custom-call | tf_op jit(solution)/shard_map/pallas_call | solution.py:60
  19.1 0.2 collective-permute-done.4.other
  19.3 1.1 %shard_map.110 = f32[4,256,128]{2,1,0:T(8,128)} custom-call(f32[64,128]{1,0:T(8,128)S(1)} %get-tuple-element.77.after.own, f32[64,128]{1,0:T(8,128)S(1)} %collective-permute-done.4.other, f32[4,256,128]{2,1,0:T(8,128)S(1)} %get-tuple-element.79.const, bf16[4,256,256]{2,1,0:T(8,128)(2,1)S(1)} %get-tuple-element.80.coef), custom_call_target="tpu_custom_call" | custom-call | tf_op jit(solution)/shard_map/pallas_call | solution.py:60
Async XLA Ops:
  3.6 1.4 %collective-permute-start = (f32[64,128]{1,0:T(8,128)S(1)}, f32[64,128]{1,0:T(8,128)S(1)}, u32[]{:S(2)}, u32[]{:S(2)}) collective-permute-start(f32[64,128]{1,0:T(8,128)S(1)} %get-tuple-element.54), channel_id=1, source_target_pairs={{0,1},{1,0},{2,3},{3,2},{4,5},{5,4},{6,7},{7,6},{8,9},{9,8},{10,11... | collective-permute-start | bytes 98312 | tf_op jit(solution)/shard_map/ppermute | solution.py:289
  5.2 4.3 %collective-permute-start.1 = (f32[64,128]{1,0:T(8,128)S(1)}, f32[64,128]{1,0:T(8,128)S(1)}, u32[]{:S(2)}, u32[]{:S(2)}) collective-permute-start(f32[64,128]{1,0:T(8,128)S(1)} %get-tuple-element.55.refs_8_.refs_13_.own), channel_id=1, source_target_pairs={{0,3},{1,2},{2,1},{3,0},{4,7},{5,6},{6,5},{7,4},{8,11},{9,10},{10,... | collective-permute-start | bytes 98312 | tf_op jit(solution)/shard_map/ppermute | solution.py:289
  9.7 3.5 %collective-permute-start.2 = (f32[64,128]{1,0:T(8,128)S(1)}, f32[64,128]{1,0:T(8,128)S(1)}, u32[]{:S(2)}, u32[]{:S(2)}) collective-permute-start(f32[64,128]{1,0:T(8,128)S(1)} %get-tuple-element.66.refs_8_.own), channel_id=1, source_target_pairs={{0,5},{1,4},{2,7},{3,6},{4,1},{5,0},{6,3},{7,2},{8,13},{9,12},{10,... | collective-permute-start | bytes 98312 | tf_op jit(solution)/shard_map/ppermute | solution.py:289
  13.4 4.4 %collective-permute-start.3 = (f32[64,128]{1,0:T(8,128)S(1)}, f32[64,128]{1,0:T(8,128)S(1)}, u32[]{:S(2)}, u32[]{:S(2)}) collective-permute-start(f32[64,128]{1,0:T(8,128)S(1)} %get-tuple-element.72.refs_8_.own), channel_id=1, source_target_pairs={{0,9},{1,8},{2,11},{3,10},{4,13},{5,12},{6,15},{7,14},{8,1},{9,0},... | collective-permute-start | bytes 98312 | tf_op jit(solution)/shard_map/ppermute | solution.py:289
  18.0 1.3 %collective-permute-start.4 = (f32[64,128]{1,0:T(8,128)S(1)}, f32[64,128]{1,0:T(8,128)S(1)}, u32[]{:S(2)}, u32[]{:S(2)}) collective-permute-start(f32[64,128]{1,0:T(8,128)S(1)} %get-tuple-element.78), channel_id=1, source_target_pairs={{0,1},{1,0},{2,3},{3,2},{4,5},{5,4},{6,7},{7,6},{8,9},{9,8},{10,11... | collective-permute-start | bytes 98312 | tf_op jit(solution)/shard_map/ppermute | solution.py:289

commit v5 on v4

--- a/solution.py
+++ b/solution.py
@@ -90,26 +90,33 @@
         copies.append(copy)
         return copy
 
-    got_b = start(rhs, rhsv)
-    got_q = start(lq, lqv)
-    got_e = start(le, lev)
-    got_node = [start(nw, nwv), start(ne, nev), start(nq, nqv)]
-    got_lw = start(lw, lwv)
+    got = {}
+    got['b'] = start(rhs, rhsv)
+    got['q'] = start(lq, lqv)
+    got['nw'] = start(nw, nwv)
+    got['w'] = start(lw, lwv)
+    got['e'] = start(le, lev)
+    got['ne'] = start(ne, nev)
+    got['nq'] = start(nq, nqv)
     got_top = [start(tq, tqv), start(te, tev), start(tw, twv)]
 
-    got_b.wait()
-    got_q.wait()
+    got['b'].wait()
+    got['q'].wait()
     mid = [split(mul_narrow(split(lqv[i]), split(rhsv[i]))) for i in range(leaves)]
-    got_e.wait()
+    got['nw'].wait()
+    got['w'].wait()
+    got['e'].wait()
     vals = []
     for i in range(leaves):
         y = mul_narrow(split(lev[i]), mid[i])
         yl[i] = y
         vals.append(split(y))
-    for copy in got_node + [got_lw]:
-        copy.wait()
-    half_maps = [split(mul(split(nwv[i].T), split(nev[i]))) for i in range(nodes)]
-    reduced = [mul_narrow(split(lwv[i].T), vals[i]) for i in range(leaves)]
+    node_wt = [split(nwv[i].T) for i in range(nodes)]
+    leaf_wt = [split(lwv[i].T) for i in range(leaves)]
+    got['ne'].wait()
+    got['nq'].wait()
+    half_maps = [split(mul(node_wt[i], split(nev[i]))) for i in range(nodes)]
+    reduced = [mul_narrow(leaf_wt[i], vals[i]) for i in range(leaves)]
     maps = [split(mul(half_maps[i], split(nqv[i]))) for i in range(nodes)]
     offset = 0
     while len(reduced) > 1:

time: 20.6 us -> 20.5 us (level)
  no operation moved by 1% of the time
where the time goes in v5:
time: 20.5 us; the launch traced here: 20.4 us
  Pallas kernels  10.5 us (51%)
  starting transfers between devices  8.34 us (41%)
  waiting for transfers between devices  1.42 us (7%)
    pallas_call x11, Pallas kernels, call(): pl.pallas_call(kernel, out_shape=[jax.ShapeDtypeStruct(s, d) for s, d in...  10.5 us
    ppermute x5, starting transfers between devices, swapped(): return lax.ppermute(value, 'leaf', pairs)  8.34 us
    ppermute x5, waiting for transfers between devices, swapped(): return lax.ppermute(value, 'leaf', pairs)  1.42 us
  transfers between devices with their start and end apart: 5, of which 4 were waited for; matrix products, arithmetic and copies ran while one was open for 0% of the time, Pallas kernels for 25%

profile of v5, /device:TPU:0, one launch (start us, length us, event | category | flops | bytes accessed | tf_op | source)
XLA Modules:
  0.0 20.4 jit_solution(15718653290617896233)
XLA Ops:
  0.0 3.6 %shard_map.100 = (f32[64,128]{1,0:T(8,128)S(1)}, f32[64,128]{1,0:T(8,128)S(1)}, f32[4,256,128]{2,1,0:T(8,128)S(1)}, f32[3,256,128]{2,1,0:T(8,128)S(1)}, f32[4,25...) custom-call(f32[4,256,128]{2,1,0:T(8,128)} %rhs.1, ...), custom_call_target="tpu_custom_call" | custom-call | tf_op jit(solution)/shard_map/pallas_call | solution.py:60
  3.6 0.6 %collective-permute-start = (f32[64,128]{1,0:T(8,128)S(1)}, f32[64,128]{1,0:T(8,128)S(1)}, u32[]{:S(2)}, u32[]{:S(2)}) collective-permute-start(f32[64,128]{1,0:T(8,128)S(1)} %get-tuple-element.54), channel_id=1, source_target_pairs={{0,1},{1,0},{2,3},{3,2},{4,5},{5,4},{6,7},{7,6},{8,9},{9,8},{10,11... | collective-permute-start | bytes 98312 | tf_op jit(solution)/shard_map/ppermute | solution.py:296
  4.1 0.8 %shard_map.101 = (bf16[256,384]{1,0:T(8,128)(2,1)S(1)}, bf16[256,384]{1,0:T(8,128)(2,1)S(1)}, f32[128,256]{1,0:T(8,128)S(1)}) custom-call(f32[4,256,256]{2,1,0:T(8,128)S(1)} %get-tuple-element.43.refs_0_, f32[4,256,256]{2,1,0:T(8,128)S(1)} %get-tuple-element.44.refs_1_, f32[4,256,128]{2,1,0:T(8,128)S(1)} %get-tuple-element.45.refs_2_), custom_call_target="tpu_custom_call" | custom-call | tf_op jit(solution)/shard_map/pallas_call | solution.py:60
  5.0 0.0 collective-permute-done.other
  5.0 0.2 shard_map.102
  5.2 2.7 %collective-permute-start.1 = (f32[64,128]{1,0:T(8,128)S(1)}, f32[64,128]{1,0:T(8,128)S(1)}, u32[]{:S(2)}, u32[]{:S(2)}) collective-permute-start(f32[64,128]{1,0:T(8,128)S(1)} %get-tuple-element.55.refs_8_.refs_13_.own), channel_id=1, source_target_pairs={{0,3},{1,2},{2,1},{3,0},{4,7},{5,6},{6,5},{7,4},{8,11},{9,10},{10,... | collective-permute-start | bytes 98312 | tf_op jit(solution)/shard_map/ppermute | solution.py:296
  7.9 1.4 %shard_map.103 = (bf16[256,384]{1,0:T(8,128)(2,1)S(1)}, bf16[256,384]{1,0:T(8,128)(2,1)S(1)}, f32[128,256]{1,0:T(8,128)S(1)}, f32[2,256,256]{2,1,0:T(8,128)S(1)}, f32[1,256,256]{2,1,0:T(8,128)S(1)}) custom-call(f32[4,256,256]{2,1,0:T(8,128)S(1)} %get-tuple-element.43.refs_0_, f32[4,256,256]{2,1,0:T(8,128)S(1)} %get-tuple-element.44.refs_1_, ...), custom_call_target="tpu_custom_call" | custom-call | tf_op jit(solution)/shard_map/pallas_call | solution.py:60
  9.3 0.2 %collective-permute-done.1.other = f32[64,128]{1,0:T(8,128)S(1)} collective-permute-done((f32[64,128]{1,0:T(8,128)S(1)}, f32[64,128]{1,0:T(8,128)S(1)}, u32[]{:S(2)}, u32[]{:S(2)}) %collective-permute-start.1) | collective-permute-done | bytes 32800 | tf_op jit(solution)/shard_map/ppermute | solution.py:296
  9.5 0.2 %shard_map.104 = (f32[64,128]{1,0:T(8,128)S(1)}, f32[64,256]{1,0:T(8,128)S(1)}) custom-call(bf16[256,384]{1,0:T(8,128)(2,1)S(1)} %get-tuple-element.61.hi, bf16[256,384]{1,0:T(8,128)(2,1)S(1)} %get-tuple-element.62.lo, f32[64,128]{1,0:T(8,128)S(1)} %get-tuple-element.55.refs_8_.refs_13_.own, f32[64,128]{1,0:T(8,128)S(1)} %collective-permute-done.1.other, ...), custom_call_target="tpu_custom_call" | custom-call | tf_op jit(solution)/shard_map/pallas_call | solution.py:60
  9.7 1.9 %collective-permute-start.2 = (f32[64,128]{1,0:T(8,128)S(1)}, f32[64,128]{1,0:T(8,128)S(1)}, u32[]{:S(2)}, u32[]{:S(2)}) collective-permute-start(f32[64,128]{1,0:T(8,128)S(1)} %get-tuple-element.66.refs_8_.own), channel_id=1, source_target_pairs={{0,5},{1,4},{2,7},{3,6},{4,1},{5,0},{6,3},{7,2},{8,13},{9,12},{10,... | collective-permute-start | bytes 98312 | tf_op jit(solution)/shard_map/ppermute | solution.py:296
  11.6 1.1 %shard_map.105 = (bf16[256,384]{1,0:T(8,128)(2,1)S(1)}, bf16[256,384]{1,0:T(8,128)(2,1)S(1)}, f32[128,256]{1,0:T(8,128)S(1)}, f32[2,256,256]{2,1,0:T(8,128)S(1)}) custom-call(f32[4,256,256]{2,1,0:T(8,128)S(1)} %get-tuple-element.43.refs_0_, f32[4,256,256]{2,1,0:T(8,128)S(1)} %get-tuple-element.44.refs_1_, f32[4,256,128]{2,1,0:T(8,128)S(1)} %get-tuple-element.45.refs_2_, ...), custom_call_target="tpu_custom_call" | custom-call | tf_op jit(solution)/shard_map/pallas_call | solution.py:60
  12.6 0.5 %collective-permute-done.2.other = f32[64,128]{1,0:T(8,128)S(1)} collective-permute-done((f32[64,128]{1,0:T(8,128)S(1)}, f32[64,128]{1,0:T(8,128)S(1)}, u32[]{:S(2)}, u32[]{:S(2)}) %collective-permute-start.2) | collective-permute-done | bytes 32800 | tf_op jit(solution)/shard_map/ppermute | solution.py:296
  13.2 0.2 shard_map.106
  13.4 2.8 %collective-permute-start.3 = (f32[64,128]{1,0:T(8,128)S(1)}, f32[64,128]{1,0:T(8,128)S(1)}, u32[]{:S(2)}, u32[]{:S(2)}) collective-permute-start(f32[64,128]{1,0:T(8,128)S(1)} %get-tuple-element.72.refs_8_.own), channel_id=1, source_target_pairs={{0,9},{1,8},{2,11},{3,10},{4,13},{5,12},{6,15},{7,14},{8,1},{9,0},... | collective-permute-start | bytes 98312 | tf_op jit(solution)/shard_map/ppermute | solution.py:296
  16.2 1.1 %shard_map.107 = (bf16[256,256]{1,0:T(8,128)(2,1)S(1)}, bf16[256,256]{1,0:T(8,128)(2,1)S(1)}, f32[2,256,256]{2,1,0:T(8,128)S(1)}) custom-call(f32[4,256,256]{2,1,0:T(8,128)S(1)} %get-tuple-element.43.refs_0_, f32[4,256,256]{2,1,0:T(8,128)S(1)} %get-tuple-element.44.refs_1_, f32[4,256,128]{2,1,0:T(8,128)S(1)} %get-tuple-element.45.refs_2_, ...), custom_call_target="tpu_custom_call" | custom-call | tf_op jit(solution)/shard_map/pallas_call | solution.py:60
  17.3 0.5 %collective-permute-done.3.other = f32[64,128]{1,0:T(8,128)S(1)} collective-permute-done((f32[64,128]{1,0:T(8,128)S(1)}, f32[64,128]{1,0:T(8,128)S(1)}, u32[]{:S(2)}, u32[]{:S(2)}) %collective-permute-start.3) | collective-permute-done | bytes 32800 | tf_op jit(solution)/shard_map/ppermute | solution.py:296
  17.8 0.2 shard_map.108
  18.0 0.4 %collective-permute-start.4 = (f32[64,128]{1,0:T(8,128)S(1)}, f32[64,128]{1,0:T(8,128)S(1)}, u32[]{:S(2)}, u32[]{:S(2)}) collective-permute-start(f32[64,128]{1,0:T(8,128)S(1)} %get-tuple-element.78), channel_id=1, source_target_pairs={{0,1},{1,0},{2,3},{3,2},{4,5},{5,4},{6,7},{7,6},{8,9},{9,8},{10,11... | collective-permute-start | bytes 98312 | tf_op jit(solution)/shard_map/ppermute | solution.py:296
  18.4 0.7 %shard_map.109 = (f32[4,256,128]{2,1,0:T(8,128)S(1)}, bf16[4,256,256]{2,1,0:T(8,128)(2,1)S(1)}) custom-call(f32[2,256,256]{2,1,0:T(8,128)S(1)} %get-tuple-element.64.refs_1_.maps_a, f32[1,256,256]{2,1,0:T(8,128)S(1)} %get-tuple-element.65.refs_2_.root_map, f32[2,256,256]{2,1,0:T(8,128)S(1)} %get-tuple-element.71.refs_1_.maps_b, ...), custom_call_target="tpu_custom_call" | custom-call | tf_op jit(solution)/shard_map/pallas_call | solution.py:60
  19.1 0.1 collective-permute-done.4.other
  19.3 1.1 %shard_map.110 = f32[4,256,128]{2,1,0:T(8,128)} custom-call(f32[64,128]{1,0:T(8,128)S(1)} %get-tuple-element.77.after.own, f32[64,128]{1,0:T(8,128)S(1)} %collective-permute-done.4.other, f32[4,256,128]{2,1,0:T(8,128)S(1)} %get-tuple-element.79.const, bf16[4,256,256]{2,1,0:T(8,128)(2,1)S(1)} %get-tuple-element.80.coef), custom_call_target="tpu_custom_call" | custom-call | tf_op jit(solution)/shard_map/pallas_call | solution.py:60
Async XLA Ops:
  3.6 1.4 %collective-permute-start = (f32[64,128]{1,0:T(8,128)S(1)}, f32[64,128]{1,0:T(8,128)S(1)}, u32[]{:S(2)}, u32[]{:S(2)}) collective-permute-start(f32[64,128]{1,0:T(8,128)S(1)} %get-tuple-element.54), channel_id=1, source_target_pairs={{0,1},{1,0},{2,3},{3,2},{4,5},{5,4},{6,7},{7,6},{8,9},{9,8},{10,11... | collective-permute-start | bytes 98312 | tf_op jit(solution)/shard_map/ppermute | solution.py:296
  5.2 4.3 %collective-permute-start.1 = (f32[64,128]{1,0:T(8,128)S(1)}, f32[64,128]{1,0:T(8,128)S(1)}, u32[]{:S(2)}, u32[]{:S(2)}) collective-permute-start(f32[64,128]{1,0:T(8,128)S(1)} %get-tuple-element.55.refs_8_.refs_13_.own), channel_id=1, source_target_pairs={{0,3},{1,2},{2,1},{3,0},{4,7},{5,6},{6,5},{7,4},{8,11},{9,10},{10,... | collective-permute-start | bytes 98312 | tf_op jit(solution)/shard_map/ppermute | solution.py:296
  9.7 3.5 %collective-permute-start.2 = (f32[64,128]{1,0:T(8,128)S(1)}, f32[64,128]{1,0:T(8,128)S(1)}, u32[]{:S(2)}, u32[]{:S(2)}) collective-permute-start(f32[64,128]{1,0:T(8,128)S(1)} %get-tuple-element.66.refs_8_.own), channel_id=1, source_target_pairs={{0,5},{1,4},{2,7},{3,6},{4,1},{5,0},{6,3},{7,2},{8,13},{9,12},{10,... | collective-permute-start | bytes 98312 | tf_op jit(solution)/shard_map/ppermute | solution.py:296
  13.4 4.4 %collective-permute-start.3 = (f32[64,128]{1,0:T(8,128)S(1)}, f32[64,128]{1,0:T(8,128)S(1)}, u32[]{:S(2)}, u32[]{:S(2)}) collective-permute-start(f32[64,128]{1,0:T(8,128)S(1)} %get-tuple-element.72.refs_8_.own), channel_id=1, source_target_pairs={{0,9},{1,8},{2,11},{3,10},{4,13},{5,12},{6,15},{7,14},{8,1},{9,0},... | collective-permute-start | bytes 98312 | tf_op jit(solution)/shard_map/ppermute | solution.py:296
  18.0 1.3 %collective-permute-start.4 = (f32[64,128]{1,0:T(8,128)S(1)}, f32[64,128]{1,0:T(8,128)S(1)}, u32[]{:S(2)}, u32[]{:S(2)}) collective-permute-start(f32[64,128]{1,0:T(8,128)S(1)} %get-tuple-element.78), channel_id=1, source_target_pairs={{0,1},{1,0},{2,3},{3,2},{4,5},{5,4},{6,7},{7,6},{8,9},{9,8},{10,11... | collective-permute-start | bytes 98312 | tf_op jit(solution)/shard_map/ppermute | solution.py:296

commit v6 on v5

--- a/solution.py
+++ b/solution.py
@@ -137,7 +137,7 @@
 
 def level_kernel(level, levels, tq, te, tw, *refs):
     first, last = level == 1, level == levels
-    outs = refs if first else refs[1:]
+    outs = refs if first else refs[2:]
     width = tw.shape[2]
     half = pl.ds(pl.multiple_of(side_of(level) * width, width), width)
     at = level - 1
@@ -147,6 +147,8 @@
         if not first:
             c = mul(split(c), split(refs[0][...]))
         outs[0][...], outs[1][...] = split(c)
+        yield
+        outs[-1][...] = mul_short(split(refs[1][...]), (outs[0][half, :], outs[1][half, :]))
         return
     e, w = split(te[at]), split(tw[at])
     x = mul(e, split(tq[at]))
@@ -168,6 +170,8 @@
         outs[i][:, :width] = a[i]
         outs[i][:, width:] = tb[i]
     outs[2][...] = -low[2 * width :]
+    yield
+    outs[3][...] = mul_short(split(refs[1][...]), (outs[0][half, :], outs[1][half, :]))
 
 
 def family(level, own, other):
@@ -176,10 +180,17 @@
     return jnp.concatenate([jnp.where(right, b, a), jnp.where(right, a, b)], axis=1)
 
 
+def product(level, hi, lo, own, other, refs):
+    if level == 1:
+        return mul_short(split(family(level, own, other)), (hi[...], lo[...]))
+    width = own.shape[1]
+    far = pl.ds(pl.multiple_of((1 - side_of(level)) * width, width), width)
+    return refs[1][...] + mul_short(split(other[...]), (hi[far, :], lo[far, :]))
+
+
 def step_kernel(level, hi, lo, own, other, *refs):
     width = own.shape[1]
-    both = split(family(level, own, other))
-    out = mul_short(both, (hi[...], lo[...]))
+    out = product(level, hi, lo, own, other, refs)
     k = out[:, width:]
     if level > 1:
         k = k + refs[0][...]
@@ -189,7 +200,7 @@
 
 def root_kernel(level, hi, lo, own, other, *refs):
     width = own.shape[1]
-    x = mul_short(split(family(level, own, other)), (hi[...], lo[...]))
+    x = product(level, hi, lo, own, other, refs)
     if level > 1:
         x = x + refs[0][...]
     right = side_of(1) == 1
@@ -331,8 +342,10 @@
         jobs = [
             (
                 functools.partial(level_kernel, level, levels),
-                [((size, wide), BF16)] * 2 + ([] if last else [((width, size), F32)]),
-                [tq, te, tw] + trans,
+                [((size, wide), BF16)] * 2
+                + ([] if last else [((width, size), F32)])
+                + ([] if level == 1 else [((cols // 2, wide), F32)]),
+                [tq, te, tw] + trans + ([] if level == 1 else [block]),
             )
         ]
         if level in plan:
@@ -346,13 +359,13 @@
                     )
                 )
         made, *chores = together(*jobs)
-        trans = made[2:]
+        trans, part = made[2:3], made[-1:] if level > 1 else []
         chores = [c[0] for c in chores]
         maps += chores
         block, k_new = call(
             functools.partial(root_kernel if last else step_kernel, level),
             [((cols // 2, width), F32), ((cols // 2, width if last else size), F32)],
-            [made[0], made[1], block, other] + k + chores,
+            [made[0], made[1], block, other] + k + part + chores,
         )
         k = [k_new]
     other = swapped(k[0], 1)

time: 20.5 us -> 20.5 us (level)
  transfers between devices with their start and end apart: 5 -> 5, of which waited for: 4 -> 4; matrix products, arithmetic and copies ran while one was open for 0% -> 0% of each run, Pallas kernels for 25% -> 26%
where the time goes in v6:
time: 20.5 us; the launch traced here: 20.3 us
  Pallas kernels  10.6 us (52%)
  starting transfers between devices  8.34 us (41%)
  waiting for transfers between devices  1.28 us (6%)
    pallas_call x11, Pallas kernels, call(): pl.pallas_call(kernel, out_shape=[jax.ShapeDtypeStruct(s, d) for s, d in...  10.6 us
    ppermute x5, starting transfers between devices, swapped(): return lax.ppermute(value, 'leaf', pairs)  8.34 us
    ppermute x5, waiting for transfers between devices, swapped(): return lax.ppermute(value, 'leaf', pairs)  1.28 us
  transfers between devices with their start and end apart: 5, of which 4 were waited for; matrix products, arithmetic and copies ran while one was open for 0% of the time, Pallas kernels for 26%

profile of v6, /device:TPU:0, one launch (start us, length us, event | category | flops | bytes accessed | tf_op | source)
XLA Modules:
  0.0 20.3 jit_solution(6098148576986252219)
XLA Ops:
  0.0 3.6 %shard_map.100 = (f32[64,128]{1,0:T(8,128)S(1)}, f32[64,128]{1,0:T(8,128)S(1)}, f32[4,256,128]{2,1,0:T(8,128)S(1)}, f32[3,256,128]{2,1,0:T(8,128)S(1)}, f32[4,25...) custom-call(f32[4,256,128]{2,1,0:T(8,128)} %rhs.1, ...), custom_call_target="tpu_custom_call" | custom-call | tf_op jit(solution)/shard_map/pallas_call | solution.py:60
  3.6 0.6 %collective-permute-start = (f32[64,128]{1,0:T(8,128)S(1)}, f32[64,128]{1,0:T(8,128)S(1)}, u32[]{:S(2)}, u32[]{:S(2)}) collective-permute-start(f32[64,128]{1,0:T(8,128)S(1)} %get-tuple-element.53), channel_id=1, source_target_pairs={{0,1},{1,0},{2,3},{3,2},{4,5},{5,4},{6,7},{7,6},{8,9},{9,8},{10,11... | collective-permute-start | bytes 98312 | tf_op jit(solution)/shard_map/ppermute | solution.py:307
  4.1 0.8 %shard_map.101 = (bf16[256,384]{1,0:T(8,128)(2,1)S(1)}, bf16[256,384]{1,0:T(8,128)(2,1)S(1)}, f32[128,256]{1,0:T(8,128)S(1)}) custom-call(f32[4,256,256]{2,1,0:T(8,128)S(1)} %get-tuple-element.46.refs_0_, f32[4,256,256]{2,1,0:T(8,128)S(1)} %get-tuple-element.47.refs_1_, f32[4,256,128]{2,1,0:T(8,128)S(1)} %get-tuple-element.48.refs_2_), custom_call_target="tpu_custom_call" | custom-call | tf_op jit(solution)/shard_map/pallas_call | solution.py:60
  5.0 0.0 collective-permute-done.other
  5.0 0.2 shard_map.102
  5.2 2.7 %collective-permute-start.1 = (f32[64,128]{1,0:T(8,128)S(1)}, f32[64,128]{1,0:T(8,128)S(1)}, u32[]{:S(2)}, u32[]{:S(2)}) collective-permute-start(f32[64,128]{1,0:T(8,128)S(1)} %get-tuple-element.54.refs_4_.refs_9_.refs_14_.own), channel_id=1, source_target_pairs={{0,3},{1,2},{2,1},{3,0},{4,7},{5,6},{6,5},{7,4},{8,11},{9,10},{10,... | collective-permute-start | bytes 98312 | tf_op jit(solution)/shard_map/ppermute | solution.py:307
  7.9 1.4 %shard_map.103 = (bf16[256,384]{1,0:T(8,128)(2,1)S(1)}, bf16[256,384]{1,0:T(8,128)(2,1)S(1)}, f32[128,256]{1,0:T(8,128)S(1)}, f32[64,384]{1,0:T(8,128)S(1)}, f32...) custom-call(f32[4,256,256]{2,1,0:T(8,128)S(1)} %get-tuple-element.46.refs_0_, ...), custom_call_target="tpu_custom_call" | custom-call | tf_op jit(solution)/shard_map/pallas_call | solution.py:60
  9.3 0.2 collective-permute-done.1.other
  9.5 0.2 shard_map.104
  9.7 1.9 %collective-permute-start.2 = (f32[64,128]{1,0:T(8,128)S(1)}, f32[64,128]{1,0:T(8,128)S(1)}, u32[]{:S(2)}, u32[]{:S(2)}) collective-permute-start(f32[64,128]{1,0:T(8,128)S(1)} %get-tuple-element.70.refs_4_.refs_9_.own), channel_id=1, source_target_pairs={{0,5},{1,4},{2,7},{3,6},{4,1},{5,0},{6,3},{7,2},{8,13},{9,12},{10,... | collective-permute-start | bytes 98312 | tf_op jit(solution)/shard_map/ppermute | solution.py:307
  11.6 1.2 %shard_map.105 = (bf16[256,384]{1,0:T(8,128)(2,1)S(1)}, bf16[256,384]{1,0:T(8,128)(2,1)S(1)}, f32[128,256]{1,0:T(8,128)S(1)}, f32[64,384]{1,0:T(8,128)S(1)}, f32[2,256,256]{2,1,0:T(8,128)S(1)}) custom-call(f32[4,256,256]{2,1,0:T(8,128)S(1)} %get-tuple-element.46.refs_0_, f32[4,256,256]{2,1,0:T(8,128)S(1)} %get-tuple-element.47.refs_1_, ...), custom_call_target="tpu_custom_call" | custom-call | tf_op jit(solution)/shard_map/pallas_call | solution.py:60
  12.7 0.4 %collective-permute-done.2.other = f32[64,128]{1,0:T(8,128)S(1)} collective-permute-done((f32[64,128]{1,0:T(8,128)S(1)}, f32[64,128]{1,0:T(8,128)S(1)}, u32[]{:S(2)}, u32[]{:S(2)}) %collective-permute-start.2) | collective-permute-done | bytes 32800 | tf_op jit(solution)/shard_map/ppermute | solution.py:307
  13.2 0.2 shard_map.106
  13.3 2.8 %collective-permute-start.3 = (f32[64,128]{1,0:T(8,128)S(1)}, f32[64,128]{1,0:T(8,128)S(1)}, u32[]{:S(2)}, u32[]{:S(2)}) collective-permute-start(f32[64,128]{1,0:T(8,128)S(1)} %get-tuple-element.77.refs_4_.refs_9_.own), channel_id=1, source_target_pairs={{0,9},{1,8},{2,11},{3,10},{4,13},{5,12},{6,15},{7,14},{8,1},{9,0},... | collective-permute-start | bytes 98312 | tf_op jit(solution)/shard_map/ppermute | solution.py:307
  16.2 1.1 %shard_map.107 = (bf16[256,256]{1,0:T(8,128)(2,1)S(1)}, bf16[256,256]{1,0:T(8,128)(2,1)S(1)}, f32[64,256]{1,0:T(8,128)S(1)}, f32[2,256,256]{2,1,0:T(8,128)S(1)}) custom-call(f32[4,256,256]{2,1,0:T(8,128)S(1)} %get-tuple-element.46.refs_0_, f32[4,256,256]{2,1,0:T(8,128)S(1)} %get-tuple-element.47.refs_1_, f32[4,256,128]{2,1,0:T(8,128)S(1)} %get-tuple-element.48.refs_2_, ...), custom_call_target="tpu_custom_call" | custom-call | tf_op jit(solution)/shard_map/pallas_call | solution.py:60
  17.3 0.5 %collective-permute-done.3.other = f32[64,128]{1,0:T(8,128)S(1)} collective-permute-done((f32[64,128]{1,0:T(8,128)S(1)}, f32[64,128]{1,0:T(8,128)S(1)}, u32[]{:S(2)}, u32[]{:S(2)}) %collective-permute-start.3) | collective-permute-done | bytes 32800 | tf_op jit(solution)/shard_map/ppermute | solution.py:307
  17.8 0.2 shard_map.108
  17.9 0.4 %collective-permute-start.4 = (f32[64,128]{1,0:T(8,128)S(1)}, f32[64,128]{1,0:T(8,128)S(1)}, u32[]{:S(2)}, u32[]{:S(2)}) collective-permute-start(f32[64,128]{1,0:T(8,128)S(1)} %get-tuple-element.84), channel_id=1, source_target_pairs={{0,1},{1,0},{2,3},{3,2},{4,5},{5,4},{6,7},{7,6},{8,9},{9,8},{10,11... | collective-permute-start | bytes 98312 | tf_op jit(solution)/shard_map/ppermute | solution.py:307
  18.4 0.7 %shard_map.109 = (f32[4,256,128]{2,1,0:T(8,128)S(1)}, bf16[4,256,256]{2,1,0:T(8,128)(2,1)S(1)}) custom-call(f32[2,256,256]{2,1,0:T(8,128)S(1)} %get-tuple-element.68.refs_2_.maps_a, f32[1,256,256]{2,1,0:T(8,128)S(1)} %get-tuple-element.69.refs_3_.root_map, f32[2,256,256]{2,1,0:T(8,128)S(1)} %get-tuple-element.76.refs_2_.maps_b, ...), custom_call_target="tpu_custom_call" | custom-call | tf_op jit(solution)/shard_map/pallas_call | solution.py:60
  19.1 0.1 collective-permute-done.4.other
  19.2 1.1 %shard_map.110 = f32[4,256,128]{2,1,0:T(8,128)} custom-call(f32[64,128]{1,0:T(8,128)S(1)} %get-tuple-element.83.after.own, f32[64,128]{1,0:T(8,128)S(1)} %collective-permute-done.4.other, f32[4,256,128]{2,1,0:T(8,128)S(1)} %get-tuple-element.85.const, bf16[4,256,256]{2,1,0:T(8,128)(2,1)S(1)} %get-tuple-element.86.coef), custom_call_target="tpu_custom_call" | custom-call | tf_op jit(solution)/shard_map/pallas_call | solution.py:60
Async XLA Ops:
  3.6 1.4 %collective-permute-start = (f32[64,128]{1,0:T(8,128)S(1)}, f32[64,128]{1,0:T(8,128)S(1)}, u32[]{:S(2)}, u32[]{:S(2)}) collective-permute-start(f32[64,128]{1,0:T(8,128)S(1)} %get-tuple-element.53), channel_id=1, source_target_pairs={{0,1},{1,0},{2,3},{3,2},{4,5},{5,4},{6,7},{7,6},{8,9},{9,8},{10,11... | collective-permute-start | bytes 98312 | tf_op jit(solution)/shard_map/ppermute | solution.py:307
  5.2 4.3 %collective-permute-start.1 = (f32[64,128]{1,0:T(8,128)S(1)}, f32[64,128]{1,0:T(8,128)S(1)}, u32[]{:S(2)}, u32[]{:S(2)}) collective-permute-start(f32[64,128]{1,0:T(8,128)S(1)} %get-tuple-element.54.refs_4_.refs_9_.refs_14_.own), channel_id=1, source_target_pairs={{0,3},{1,2},{2,1},{3,0},{4,7},{5,6},{6,5},{7,4},{8,11},{9,10},{10,... | collective-permute-start | bytes 98312 | tf_op jit(solution)/shard_map/ppermute | solution.py:307
  9.7 3.5 %collective-permute-start.2 = (f32[64,128]{1,0:T(8,128)S(1)}, f32[64,128]{1,0:T(8,128)S(1)}, u32[]{:S(2)}, u32[]{:S(2)}) collective-permute-start(f32[64,128]{1,0:T(8,128)S(1)} %get-tuple-element.70.refs_4_.refs_9_.own), channel_id=1, source_target_pairs={{0,5},{1,4},{2,7},{3,6},{4,1},{5,0},{6,3},{7,2},{8,13},{9,12},{10,... | collective-permute-start | bytes 98312 | tf_op jit(solution)/shard_map/ppermute | solution.py:307
  13.3 4.4 %collective-permute-start.3 = (f32[64,128]{1,0:T(8,128)S(1)}, f32[64,128]{1,0:T(8,128)S(1)}, u32[]{:S(2)}, u32[]{:S(2)}) collective-permute-start(f32[64,128]{1,0:T(8,128)S(1)} %get-tuple-element.77.refs_4_.refs_9_.own), channel_id=1, source_target_pairs={{0,9},{1,8},{2,11},{3,10},{4,13},{5,12},{6,15},{7,14},{8,1},{9,0},... | collective-permute-start | bytes 98312 | tf_op jit(solution)/shard_map/ppermute | solution.py:307
  17.9 1.3 %collective-permute-start.4 = (f32[64,128]{1,0:T(8,128)S(1)}, f32[64,128]{1,0:T(8,128)S(1)}, u32[]{:S(2)}, u32[]{:S(2)}) collective-permute-start(f32[64,128]{1,0:T(8,128)S(1)} %get-tuple-element.84), channel_id=1, source_target_pairs={{0,1},{1,0},{2,3},{3,2},{4,5},{5,4},{6,7},{7,6},{8,9},{9,8},{10,11... | collective-permute-start | bytes 98312 | tf_op jit(solution)/shard_map/ppermute | solution.py:307
